TPU v7x, 256 devices: a whole 4x4x8 slice. The times are simulated.
256 devices in a mesh: expert: 32 (over z_hi, y, core), dp: 8 (over z_lo, x).
Axes of the slice: x: 4, y: 4, z: 8 (z_hi: 4, z_lo: 2; z = z_hi * 2 + z_lo), core: 2. Of those that a mesh axis runs over, the one named last changes fastest.
Arguments:
- tokens: bfloat16 [32768, 4096], P(('expert', 'dp')), may hold values from -6 to 6
- route: int32 [32768, 2], P(('expert', 'dp')), may hold values from 0 to 63, all different within a row; in each aligned block of 128 rows (0 to 127, 128 to 255, ...) at most 12 rows name the same one
- gate_output_gradient: bfloat16 [32768, 2, 1536], P(('expert', 'dp')), may hold values from -0.4375 to 0.4375
- frozen_gate_weight: bfloat16 [64, 4096, 1536], P('expert', 'dp'), may hold values from -0.09375 to 0.09375
- adapter_first: bfloat16 [64, 4096, 16], P('expert'), may hold values from -0.09375 to 0.09375
- adapter_second: bfloat16 [64, 16, 1536], P('expert'), may hold values from -0.15625 to 0.15625
Outputs:
- grad_a: float32 [64, 4096, 16], P('expert')
- grad_b: float32 [64, 16, 1536], P('expert')
Inputs may be any that keep to these rules, and one draw needn't show every extreme that they name: `route`: each row names 2 different experts. Within each device's aligned block of 128 rows no expert is named more than 12 times.
All inputs are finite; a program needn't handle non-finite values.
Results may differ from a plain program's by a relative error of at most 0.0043.
Values may be sent and summed in bfloat16 or wider, within the bound.
No kernel may reach another device: no remote copies, remote signals or barrier semaphores. Data moves between devices by JAX's collectives and lax.ppermute only.
A program may use at most 128 MiB of HBM per device.

v0:
```python
import jax
import jax.numpy as jnp
from jax import lax
from jax.sharding import PartitionSpec as P

ADAPTER_SCALE = 2.0


def silu_slope(gate_preactivation):
    squash = jax.nn.sigmoid(gate_preactivation)
    return squash * (1.0 + gate_preactivation * (1.0 - squash))


def block_product(input_rows, piece):
    return jnp.dot(input_rows, piece, preferred_element_type=jnp.float32)


def prepare(input_rows, rows_g):
    block = 128
    return (input_rows, rows_g, None, block)


def adapter_grads(input_rows, rows_g, frozen_output, first_adapter_factor, second_adapter_factor):
    rank_reduced_output = jnp.dot(
        input_rows, first_adapter_factor, preferred_element_type=jnp.float32
    ).astype(jnp.bfloat16)
    gate_preactivation = frozen_output + ADAPTER_SCALE * jnp.dot(
        rank_reduced_output, second_adapter_factor, preferred_element_type=jnp.float32
    )
    activation_slope = (rows_g.astype(jnp.float32) * silu_slope(gate_preactivation)).astype(
        jnp.bfloat16
    )
    up_gradient = ADAPTER_SCALE * jnp.einsum(
        "nr,nf->rf", rank_reduced_output, activation_slope, preferred_element_type=jnp.float32
    )
    rank_backward = jnp.einsum(
        "nf,rf->nr", activation_slope, second_adapter_factor, preferred_element_type=jnp.float32
    ).astype(jnp.bfloat16)
    down_gradient = ADAPTER_SCALE * jnp.einsum(
        "nd,nr->dr", input_rows, rank_backward, preferred_element_type=jnp.float32
    )
    return (down_gradient, up_gradient)


def local(tokens, route, gate_output_gradient, frozen_gate_weight, adapter_first, adapter_second):
    experts_here = frozen_gate_weight.shape[0]
    columns = lax.axis_size("expert")
    experts = experts_here * columns
    tok_rows = tokens.shape[0]
    top_count = route.shape[1]
    width = tokens.shape[1]
    hidden = gate_output_gradient.shape[2]
    capacity = 3 * tok_rows * top_count // experts
    slot_count = tok_rows * top_count
    flat_route = route.reshape(slot_count)
    labels = jnp.arange(experts, dtype=jnp.int32)
    one_hot = (flat_route[:, None] == labels[None, :]).astype(jnp.int32)
    ranks = jnp.sum((jnp.cumsum(one_hot, axis=0) - one_hot) * one_hot, axis=1)
    target = (flat_route % experts_here * columns + flat_route // experts_here) * capacity + ranks
    positions = jnp.arange(experts * capacity, dtype=jnp.int32)
    hits = target[None, :] == positions[:, None]
    filled = jnp.any(hits, axis=1)
    slot_ids = jnp.arange(slot_count, dtype=jnp.int32)
    source_slot = jnp.sum(jnp.where(hits, slot_ids[None, :], 0), axis=1)
    send_x = tokens[source_slot // top_count].reshape(experts_here, columns, capacity, width)
    flat_grad = gate_output_gradient.reshape(slot_count, hidden)
    send_g = jnp.where(
        filled[:, None], flat_grad[source_slot], jnp.zeros((), gate_output_gradient.dtype)
    )
    send_g = send_g.reshape(experts_here, columns, capacity, hidden)
    group_rows = columns * capacity
    recv_x, recv_g = (
        lax.all_to_all(send_x, "expert", split_axis=1, concat_axis=1, tiled=True),
        lax.all_to_all(send_g, "expert", split_axis=1, concat_axis=1, tiled=True),
    )
    input_rows = recv_x.reshape(experts_here, group_rows, width)
    rows_g = recv_g.reshape(experts_here, group_rows, hidden)
    ready_inputs = [
        prepare(input_rows[local_result], rows_g[local_result])
        for local_result in range(experts_here)
    ]

    def add_rows(piece):
        return jnp.stack(
            [
                block_product(ready_inputs[local_result][0], piece[local_result])
                for local_result in range(experts_here)
            ]
        )

    frozen_output = add_rows(lax.all_gather(frozen_gate_weight, "dp", axis=1, tiled=True))
    results = [
        adapter_grads(
            ready_inputs[local_result][0],
            ready_inputs[local_result][1],
            frozen_output[local_result],
            adapter_first[local_result],
            adapter_second[local_result],
        )
        for local_result in range(experts_here)
    ]
    grad_a_local = jnp.stack([result[0] for result in results])
    grad_b_local = jnp.stack([result[1] for result in results])
    grad_a, grad_b = lax.psum((grad_a_local, grad_b_local), "dp")
    return (grad_a, grad_b)


def solution(mesh):
    return jax.shard_map(
        local,
        mesh=mesh,
        in_specs=(
            P(("expert", "dp"), None),
            P(("expert", "dp"), None),
            P(("expert", "dp"), None, None),
            P("expert", "dp", None),
            P("expert", None, None),
            P("expert", None, None),
        ),
        out_specs=(P("expert", None, None), P("expert", None, None)),
        check_vma=False,
    )
```

profile of v0, /device:TPU:8, one launch (start us, length us, event | category | flops | bytes accessed | tf_op | source)
XLA Modules:
  0.0 568.3 jit_solution(11198235258273988007)
XLA Ops:
  7.2 0.7 all-gather.2.cloned.1.call-update
  9.9 3.9 gather_fusion.1
  13.7 4.8 gather.10
  18.8 2.2 broadcast_select_fusion
  21.0 3.8 copy.20
  24.8 11.7 %all-to-all-start.1 = ((bf16[2,32,12,1536]{3,0,2,1:T(2,128)(2,1)}), bf16[2,32,12,1536]{3,0,2,1:T(2,128)(2,1)S(1)}, u32[]{:S(2)}, u32[]{:S(2)}) async-start(bf16[2,32,12,1536]{3,0,2,1:T(2,128)(2,1)} %copy.20), calls=%async_computation.1 | async-start | bytes 4718592 | tf_op jit(solution)/shard_map/all_to_all | solution.py:74
  36.6 5.7 gather_fusion
  42.2 9.8 %reshape.176 = bf16[2,32,12,4096]{3,2,1,0:T(8,128)(2,1)} reshape(bf16[768,4096]{1,0:T(8,128)(2,1)} %gather_fusion) | data formatting | bytes 12582912 | tf_op jit(solution)/shard_map/reshape | solution.py:65
  52.0 13.6 %copy.19 = bf16[2,32,12,4096]{3,0,2,1:T(2,128)(2,1)} copy(bf16[2,32,12,4096]{3,2,1,0:T(8,128)(2,1)} %reshape.176) | data formatting | bytes 12582912 | tf_op jit(solution)/shard_map/reshape | solution.py:65
  65.5 53.0 %all-to-all-done.1 = bf16[2,32,12,1536]{3,0,2,1:T(2,128)(2,1)S(1)} async-done(((bf16[2,32,12,1536]{3,0,2,1:T(2,128)(2,1)}), bf16[2,32,12,1536]{3,0,2,1:T(2,128)(2,1)S(1)}, u32[]{:S(2)}, u32[]{:S(2)}) %all-to-all-start.1) | async-done | bytes 2359328 | tf_op jit(solution)/shard_map/all_to_all | solution.py:74
  118.6 5.3 all-to-all-start
  124.0 15.2 %fusion.7 = (f32[32,12,1536]{2,1,0:T(8,128)}, f32[32,12,1536]{2,1,0:T(8,128)}) fusion(bf16[2,32,12,1536]{3,0,2,1:T(2,128)(2,1)S(1)} %all-to-all-done.1), kind=kLoop, calls=%fused_computation.20 | loop fusion | flops 1179648 | bytes 7077888 | tf_op jit(solution)/shard_map/convert_element_type | solution.py:30
  139.1 3.6 reshape.178
  142.7 3.6 reshape.179
  146.2 186.4 %all-to-all-done = bf16[2,32,12,4096]{3,0,2,1:T(2,128)(2,1)} async-done(((bf16[2,32,12,4096]{3,0,2,1:T(2,128)(2,1)}), bf16[2,32,12,4096]{3,0,2,1:T(2,128)(2,1)}, u32[]{:S(2)}, u32[]{:S(2)}) %all-to-all-start) | async-done | bytes 6291488 | tf_op jit(solution)/shard_map/all_to_all | solution.py:73
  332.6 33.0 %slice_reduce_fusion.1 = (bf16[32,12,4096]{2,1,0:T(8,128)(2,1)}, bf16[32,12,4096]{2,1,0:T(8,128)(2,1)}) fusion(bf16[2,32,12,4096]{3,0,2,1:T(2,128)(2,1)} %all-to-all-done), kind=kLoop, calls=%fused_computation.7 | loop fusion | bytes 12582912 | tf_op jit(solution)/shard_map/slice | solution.py:79
  365.6 5.6 squeeze.26
  371.2 5.6 squeeze.30
  376.8 3.0 convolution_convert_fusion.3
  379.8 0.9 convolution_convert_fusion.1
  380.8 69.1 %all-gather.2.cloned.1.call-done = bf16[2,4096,1536]{2,1,0:T(8,128)(2,1)} async-done(((bf16[2,512,1536]{2,1,0:T(8,128)(2,1)}), bf16[2,4096,1536]{2,1,0:T(8,128)(2,1)}) %all-gather.2.cloned.1.call-update) | async-done | bytes 25165840 | tf_op jit(solution)/shard_map/all_gather | solution.py:91
  449.8 9.3 %fusion.1 = f32[384,1536]{1,0:T(8,128)S(1)} fusion(bf16[384,4096]{1,0:T(8,128)(2,1)} %squeeze.26, bf16[2,4096,1536]{2,1,0:T(8,128)(2,1)} %all-gather.2.cloned.1.call-done), kind=kOutput, calls=%fused_computation.5 | convolution fusion | flops 4831838208 | bytes 18087936 | tf_op jit(solution)/shard_map/dot_general | solution.py:15
  459.2 1.1 multiply_convert_fusion.1
  460.6 3.0 fusion.3
  463.6 9.1 %fusion = f32[384,1536]{1,0:T(8,128)S(1)} fusion(bf16[384,4096]{1,0:T(8,128)(2,1)} %squeeze.30, bf16[2,4096,1536]{2,1,0:T(8,128)(2,1)} %all-gather.2.cloned.1.call-done), kind=kOutput, calls=%fused_computation.3 | convolution fusion | flops 4831838208 | bytes 18087936 | tf_op jit(solution)/shard_map/dot_general | solution.py:15
  472.7 1.1 multiply_convert_fusion
  474.1 3.1 fusion.2
  477.2 0.7 pad_maximum_fusion.1
  477.9 0.8 pad_maximum_fusion
  478.7 79.3 %all-reduce.3.cloned.1.call-done = (f32[2,4096,16]{1,2,0:T(8,128)}, f32[2,16,1536]{2,1,0:T(8,128)}) async-done(((f32[2,4096,16]{1,2,0:T(8,128)}, f32[2,16,1536]{2,1,0:T(8,128)}), (f32[2,4096,16]{1,2,0:T(8,128)}, f32[2,16,1536]{2,1,0:T(8,128)})) %all-reduce.3.cloned.1.call-update) | async-done | bytes 720912 | tf_op jit(solution)/shard_map/psum | solution.py:104
  558.0 1.9 copy.29
  559.9 1.6 copy.30
  (39 shorter events, 2.9 us)
Async XLA Ops:
  7.2 29.4 %copy-start = (bf16[128,4096]{1,0:T(8,128)(2,1)S(1)}, bf16[128,4096]{1,0:T(8,128)(2,1)}, u32[]{:S(2)}) copy-start(bf16[128,4096]{1,0:T(8,128)(2,1)} %param.6) | copy-start | bytes 3145732
  7.2 0.8 copy-start.8
  7.2 2.0 copy-start.5
  7.2 442.6 %all-gather.2.cloned.1.call-start = ((), (), s32[]{:S(2)}) async-start(), calls=%async_computation.2 | async-start | bytes 28311552 | tf_op jit(solution)/shard_map/all_gather | solution.py:91
  24.8 93.7 %all-to-all-start.1 = ((bf16[2,32,12,1536]{3,0,2,1:T(2,128)(2,1)}), bf16[2,32,12,1536]{3,0,2,1:T(2,128)(2,1)S(1)}, u32[]{:S(2)}, u32[]{:S(2)}) async-start(bf16[2,32,12,1536]{3,0,2,1:T(2,128)(2,1)} %copy.20), calls=%async_computation.1 | async-start | bytes 4718592 | tf_op jit(solution)/shard_map/all_to_all | solution.py:74
  118.6 214.0 %all-to-all-start = ((bf16[2,32,12,4096]{3,0,2,1:T(2,128)(2,1)}), bf16[2,32,12,4096]{3,0,2,1:T(2,128)(2,1)}, u32[]{:S(2)}, u32[]{:S(2)}) async-start(bf16[2,32,12,4096]{3,0,2,1:T(2,128)(2,1)} %copy.19), calls=%async_computation | async-start | bytes 12582912 | tf_op jit(solution)/shard_map/all_to_all | solution.py:73
  123.9 434.1 %all-reduce.3.cloned.1.call-start = ((), (), s32[]{:S(2)}) async-start(), calls=%async_computation.3 | async-start | bytes 1441792 | tf_op jit(solution)/shard_map/psum | solution.py:104
  371.2 5.6 copy-start.6
  376.8 3.0 copy-start.2
  380.8 78.4 %copy-start.7 = (bf16[2,16,1536]{2,1,0:T(8,128)(2,1)S(1)}, bf16[2,16,1536]{2,1,0:T(8,128)(2,1)}, u32[]{:S(2)}) copy-start(bf16[2,16,1536]{2,1,0:T(8,128)(2,1)} %param.11) | copy-start | bytes 294916
  449.8 9.3 %copy-start.4 = (f32[384,1536]{1,0:T(8,128)S(1)}, f32[384,1536]{1,0:T(8,128)}, u32[]{:S(2)}) copy-start(f32[384,1536]{1,0:T(8,128)} %reshape.178) | copy-start | bytes 7077892
  463.6 9.1 %copy-start.3 = (f32[384,1536]{1,0:T(8,128)S(1)}, f32[384,1536]{1,0:T(8,128)}, u32[]{:S(2)}) copy-start(f32[384,1536]{1,0:T(8,128)} %reshape.179) | copy-start | bytes 7077892
  474.1 87.4 %copy-start.1 = (bf16[128,4096]{1,0:T(8,128)(2,1)S(1)}, bf16[128,4096]{1,0:T(8,128)(2,1)}, u32[]{:S(2)}) copy-start(bf16[128,4096]{1,0:T(8,128)(2,1)} %param.6) | copy-start | bytes 3145732
Sparse Core Ops, SparseCore 0:
  9.8 439.9 all-gather.1
  478.8 79.1 all-reduce.2
where the time goes:
time: 569 us; the launch traced here: 568 us
  waiting for transfers between devices  388 us (68%)
  local copies, waits for them, and re-layouts  97.3 us (17%)
  matrix products  31.2 us (5%)
  other arithmetic  20 us (4%)
  starting transfers between devices  17.1 us (3%)
  between operations  14.2 us (2%)
    all_to_all x1, waiting for transfers between devices, local(): lax.all_to_all(send_x, 'expert', split_axis=1, concat_axis=1, tiled=True)  186 us
    psum x1, waiting for transfers between devices, local(): grad_a, grad_b = lax.psum((grad_a_local, grad_b_local), 'dp')  79.3 us
    all_gather x1, waiting for transfers between devices, local(): lax.all_gather(frozen_gate_weight, 'dp', axis=1, tiled=True)  69.1 us
    all_to_all x1, waiting for transfers between devices, local(): lax.all_to_all(send_g, 'expert', split_axis=1, concat_axis=1, tiled=True)  53 us
    slice x1, local copies, waits for them, and re-layouts, local(): input_rows[local_result]  33 us
    reshape x2, local copies, waits for them, and re-layouts, local(): tokens[source_slot // top_count]  23.3 us
    dot_general x2, matrix products, block_product(): return jnp.dot(input_rows, piece, preferred_element_type=jnp.float32)  18.4 us
    convert_element_type x1, other arithmetic, adapter_grads(): rows_g.astype(jnp.float32) * silu_slope(gate_preactivation)  15.2 us
  transfers between devices with their start and end apart: 4, of which 4 were waited for; matrix products, arithmetic and copies ran while one was open for 20% of the time, Pallas kernels for 0%

commit v1 on v0

v1 whole, which is shorter than its diff:
```python
import jax
import jax.numpy as jnp
from jax import lax
from jax.sharding import Mesh, PartitionSpec as P

ADAPTER_SCALE = 2.0
EXPERT_AXES = ("zh", "y", "c")
DP_AXES = ("zl", "x")
PLANE = ("zh", "y", "c", "zl")


def dot(a, b, dims=((1,), (0,))):
    return lax.dot_general(a, b, (dims, ((), ())), preferred_element_type=jnp.float32)


def silu_slope(gate_preactivation):
    squash = jax.nn.sigmoid(gate_preactivation)
    return squash * (1.0 + gate_preactivation * (1.0 - squash))


def slot_targets(route, cap):
    rows, top = route.shape
    flat = route.T.reshape(rows * top)
    before = jnp.arange(rows * top)[:, None] > jnp.arange(rows * top)[None, :]
    same = flat[:, None] == flat[None, :]
    ranks = jnp.sum((same & before).astype(jnp.int32), axis=1)
    return (flat * cap + ranks).reshape(top, rows)


def send_places(experts, cap, swap):
    p = jnp.arange(experts * 24, dtype=jnp.int32)
    e, piece, r = p // 24, p % 24 // 8, p % 8
    rank = jnp.where(piece < 2, r, 8 + r % 4)
    half = jnp.where(piece < 2, piece, r // 4)
    if swap:
        half = jnp.where(e % 2 == 1, 1 - half, half)
    return e * cap + rank, half


def local(tokens, route, gate_output_gradient, frozen_gate_weight, adapter_first, adapter_second):
    tok_rows, width = tokens.shape
    hidden = gate_output_gradient.shape[2]
    experts = 64
    cap = 12
    zl = lax.axis_index("zl")

    mine = lax.dynamic_index_in_dim(frozen_gate_weight, zl, 0, keepdims=False)
    other = lax.dynamic_index_in_dim(frozen_gate_weight, 1 - zl, 0, keepdims=False)
    weight_near = lax.all_gather(mine, "x", axis=0, tiled=True)
    got = lax.ppermute(other, "zl", [(0, 1), (1, 0)])
    weight_far = lax.all_gather(got, "x", axis=0, tiled=True)
    first = lax.dynamic_index_in_dim(adapter_first, zl, 0, keepdims=False)
    second = lax.dynamic_index_in_dim(adapter_second, zl, 0, keepdims=False)
    half_width = width // 2
    first = jnp.where(zl == 0, first, jnp.roll(first, half_width, axis=0))

    target = slot_targets(route, cap)
    place, half = send_places(experts, cap, True)
    match = (place[:, None] == target[0][None, :]) | (place[:, None] == target[1][None, :])
    pick = jnp.concatenate([match & (half == 0)[:, None], match & (half == 1)[:, None]], axis=1)
    stack = jnp.concatenate([tokens[:, :half_width], tokens[:, half_width:]], axis=0)
    send_x = dot(pick.astype(jnp.bfloat16), stack).astype(jnp.bfloat16)
    send_x = send_x.reshape(experts, 24, half_width)
    recv_x = lax.all_to_all(send_x, PLANE, split_axis=0, concat_axis=0, tiled=True)

    place, half = send_places(experts, cap, False)
    match = place[:, None] == target.reshape(1, 2 * tok_rows)
    pick = jnp.concatenate([match & (half == 0)[:, None], match & (half == 1)[:, None]], axis=1)
    half_hidden = hidden // 2
    parts = [
        gate_output_gradient[:, k, h * half_hidden : (h + 1) * half_hidden]
        for h in range(2)
        for k in range(2)
    ]
    send_g = dot(pick.astype(jnp.bfloat16), jnp.concatenate(parts, axis=0)).astype(jnp.bfloat16)
    send_g = send_g.reshape(experts, 24, half_hidden)
    recv_g = lax.all_to_all(send_g, PLANE, split_axis=0, concat_axis=0, tiled=True)

    row = jnp.arange(4 * experts)
    col = jnp.arange(8 * experts)
    same_source = (row // 4)[:, None] == (col // 8)[None, :]

    def gather_half(received, h):
        main = received[:, 8 * h : 8 * h + 8].reshape(8 * experts, -1)
        tail = received[:, 16:24].reshape(8 * experts, -1)
        pick = same_source & ((4 * h + row % 4)[:, None] == (col % 8)[None, :])
        tail = dot(pick.astype(jnp.bfloat16), tail).astype(jnp.bfloat16)
        return jnp.concatenate([main, tail], axis=0)

    x_near = gather_half(recv_x, 0)
    x_far = gather_half(recv_x, 1)
    low = (dot(x_near, first[:half_width]) + dot(x_far, first[half_width:])).astype(jnp.bfloat16)
    frozen = dot(x_near, weight_near) + dot(x_far, weight_far)
    preact = frozen + ADAPTER_SCALE * dot(low, second)
    rows_g = jnp.concatenate([gather_half(recv_g, 0), gather_half(recv_g, 1)], axis=1)
    slope = (rows_g.astype(jnp.float32) * silu_slope(preact)).astype(jnp.bfloat16)
    back = dot(slope, second, ((1,), (1,))).astype(jnp.bfloat16)
    grads = ADAPTER_SCALE * jnp.concatenate(
        [
            dot(back, x_near, ((0,), (0,))),
            dot(back, x_far, ((0,), (0,))),
            dot(low, slope, ((0,), (0,))),
        ],
        axis=1,
    )

    rank = grads.shape[0]
    chunk = grads.shape[1] // 4
    parts = grads.reshape(rank, 4, chunk).transpose(1, 0, 2)
    parts = lax.all_to_all(parts, "x", split_axis=0, concat_axis=0, tiled=True)
    total = jnp.sum(parts, axis=0).astype(jnp.bfloat16)
    total = jnp.broadcast_to(total[None], (8, rank, chunk))
    total = lax.all_to_all(total, DP_AXES, split_axis=0, concat_axis=0, tiled=True)
    total = total.reshape(2, 4, rank, chunk).transpose(0, 2, 1, 3).reshape(2, rank, 4 * chunk)
    near, far = total[:, :, :half_width], total[:, :, half_width:width]
    grad_a = jnp.stack(
        [
            jnp.concatenate([near[0], far[0]], axis=1),
            jnp.concatenate([far[1], near[1]], axis=1),
        ]
    )
    grad_a = grad_a.transpose(0, 2, 1).astype(jnp.float32)
    return grad_a, total[:, :, width:].astype(jnp.float32)


def solution(mesh):
    fine = Mesh(mesh.devices.reshape(4, 4, 2, 2, 4), EXPERT_AXES + DP_AXES)
    everyone = EXPERT_AXES + DP_AXES
    return jax.shard_map(
        local,
        mesh=fine,
        in_specs=(
            P(everyone, None),
            P(everyone, None),
            P(everyone, None, None),
            P(EXPERT_AXES, DP_AXES, None),
            P(EXPERT_AXES, None, None),
            P(EXPERT_AXES, None, None),
        ),
        out_specs=(P(EXPERT_AXES, None, None), P(EXPERT_AXES, None, None)),
        check_vma=False,
    )
```

time: 569 us -> 376 us (0.66)
  waiting for transfers between devices: 388 us -> 259 us
  local copies, waits for them, and re-layouts: 97.3 us -> 11.2 us
  blocking collectives: 0 us -> 22.1 us
  other arithmetic: 20 us -> 6.15 us
  matrix products: 31.2 us -> 43.6 us
    all_to_all x2, waiting for transfers between devices: 239 us -> 46.8 us  [the longest x1 46.8 us: local(): lax.all_to_all(send_g, PLANE, split_axis=0, concat_axis=0, tiled=True)]
    ppermute x0 -> x1, waiting for transfers between devices: none -> 169 us  [local(): got = lax.ppermute(other, 'zl', [(0, 1), (1, 0)])]
    psum x1 -> x0, waiting for transfers between devices: 79.3 us -> none  [local(): grad_a, grad_b = lax.psum((grad_a_local, grad_b_local), 'dp')]
    slice x2 -> x4, local copies, waits for them, and re-layouts: 33.2 us -> 2.85 us  [the longest x1 2.75 us: local(): gate_output_gradient[:, k, h * half_hidden:(h + 1) * half_hidden]]
    all_gather x1 -> x2, waiting for transfers between devices: 69.1 us -> 42.7 us  [the longest x1 42.7 us: local(): weight_far = lax.all_gather(got, 'x', axis=0, tiled=True)]
    all_to_all x0 -> x2, blocking collectives: none -> 22.1 us  [the longest x1 11.1 us: local(): lax.all_to_all(total, DP_AXES, split_axis=0, concat_axis=0, tiled=True)]
    reshape x4 -> x3, local copies, waits for them, and re-layouts: 23.8 us -> 4.09 us  [the longest x2 4.06 us: gather_half(): main = received[:, 8 * h:8 * h + 8].reshape(8 * experts, -1)]
    gather x3 -> x0, local copies, waits for them, and re-layouts: 14.3 us -> none  [the longest x2 8.63 us: local(): flat_grad[source_slot]]
  transfers between devices with their start and end apart: 4 -> 5, of which waited for: 4 -> 3; matrix products, arithmetic and copies ran while one was open for 20% -> 9% of each run, Pallas kernels for 0% -> 0%
where the time goes in v1:
time: 376 us
  waiting for transfers between devices  259 us (69%)
  matrix products  43.6 us (12%)
  blocking collectives  22.1 us (6%)
  starting transfers between devices  19.7 us (5%)
  between operations  14.3 us (4%)
  local copies, waits for them, and re-layouts  11.2 us (3%)
  other arithmetic  6.15 us (2%)
    ppermute x1, waiting for transfers between devices, local(): got = lax.ppermute(other, 'zl', [(0, 1), (1, 0)])  169 us
    all_to_all x1, waiting for transfers between devices, local(): lax.all_to_all(send_g, PLANE, split_axis=0, concat_axis=0, tiled=True)  46.8 us
    dot_general x15, matrix products, dot(): lax.dot_general(a, b, (dims, ((), ())), preferred_element_type=jnp.float32)  43.6 us
    all_gather x1, waiting for transfers between devices, local(): weight_far = lax.all_gather(got, 'x', axis=0, tiled=True)  42.7 us
    all_to_all x1, starting transfers between devices, local(): lax.all_to_all(send_g, PLANE, split_axis=0, concat_axis=0, tiled=True)  12.1 us
    all_to_all x1, blocking collectives, local(): lax.all_to_all(total, DP_AXES, split_axis=0, concat_axis=0, tiled=True)  11.1 us
    all_to_all x1, blocking collectives, local(): parts = lax.all_to_all(parts, 'x', split_axis=0, concat_axis=0, tiled=True)  11 us
  transfers between devices with their start and end apart: 5, of which 3 were waited for; matrix products, arithmetic and copies ran while one was open for 9% of the time, Pallas kernels for 0%

profile of v1, /device:TPU:8, one launch (start us, length us, event | category | flops | bytes accessed | tf_op | source)
XLA Modules:
  0.0 375.5 jit_solution(1847218579089179131)
XLA Ops:
  7.2 0.9 convert_reduce_fusion
  8.2 0.7 multiply_add_fusion
  8.9 2.8 fusion.96
  11.7 1.4 compare_and_fusion.1
  13.2 2.9 convolution_convert_fusion.1
  16.0 12.1 %all-to-all-start = ((bf16[64,24,768]{2,1,0:T(8,128)(2,1)}), bf16[64,24,768]{2,1,0:T(8,128)(2,1)S(1)}, u32[]{:S(2)}, u32[]{:S(2)}) async-start(bf16[64,24,768]{2,1,0:T(8,128)(2,1)} %bitcast.80), calls=%async_computation | async-start | bytes 4718592 | tf_op jit(solution)/shard_map/all_to_all | solution.py:77
  28.2 3.9 %dynamic-slice_bitcast_fusion = (bf16[512,1536]{1,0:T(8,128)(2,1)}, bf16[1,512,1536]{2,1,0:T(8,128)(2,1)}) fusion(bf16[2,512,1536]{2,1,0:T(8,128)(2,1)} %param.9, s32[]{:T(128)S(6)} %select_n.335, s32[]{:T(128)S(6)} %select_n.334), kind=kLoop, calls=%fused_computation.17 | loop fusion | bytes 6291464 | tf_op jit(solution)/shard_map/jit(dynamic_index_in_dim)/squeeze | solution.py:48
  32.2 1.4 fusion.23
  33.7 4.5 %convolution_convert_fusion = bf16[1536,2048]{1,0:T(8,128)(2,1)} fusion(pred[1536,128]{1,0:T(32,128)(4,1)S(1)} %get-tuple-element.23, pred[1536,128]{1,0:T(32,128)(4,1)S(1)} %get-tuple-element.22, bf16[128,2048]{1,0:T(8,128)(2,1)S(1)} %get-tuple-element.9, bf16[128,2048]{1,0:T(8,128)(2,1)S(1)} %get-tuple-element.8), kind=kOutput, calls=%fused_computation | convolution fusion | flops 1616248832 | bytes 7733248 | tf_op jit(solution)/shard_map/dot_general | solution.py:13
  38.1 46.8 %all-to-all-done = bf16[64,24,768]{2,1,0:T(8,128)(2,1)S(1)} async-done(((bf16[64,24,768]{2,1,0:T(8,128)(2,1)}), bf16[64,24,768]{2,1,0:T(8,128)(2,1)S(1)}, u32[]{:S(2)}, u32[]{:S(2)}) %all-to-all-start) | async-done | bytes 2359328 | tf_op jit(solution)/shard_map/all_to_all | solution.py:77
  84.9 5.8 %all-to-all-start.1 = ((bf16[64,24,2048]{2,1,0:T(8,128)(2,1)}), bf16[64,24,2048]{2,1,0:T(8,128)(2,1)}, u32[]{:S(2)}, u32[]{:S(2)}) async-start(bf16[64,24,2048]{2,1,0:T(8,128)(2,1)} %bitcast.79), calls=%async_computation.1 | async-start | bytes 12582912 | tf_op jit(solution)/shard_map/all_to_all | solution.py:64
  90.8 1.7 collective-permute-start
  92.5 169.0 %collective-permute-done = bf16[512,1536]{1,0:T(8,128)(2,1)} collective-permute-done((bf16[512,1536]{1,0:T(8,128)(2,1)}, bf16[512,1536]{1,0:T(8,128)(2,1)}, u32[]{:S(2)}, u32[]{:S(2)}) %collective-permute-start) | collective-permute-done | bytes 1572896 | tf_op jit(solution)/shard_map/ppermute | solution.py:50
  261.6 1.2 convolution_convert_fusion.5
  262.8 1.2 convolution_convert_fusion.4
  264.0 1.1 slice_bitcast_fusion.7
  265.1 2.4 convolution_convert_fusion.3
  267.4 3.0 slice_bitcast_fusion
  270.5 0.9 fusion.14
  271.4 2.4 convolution_convert_fusion.2
  273.8 0.9 fusion.8
  274.8 2.9 fusion.44
  277.7 9.7 %fusion = f32[768,1536]{1,0:T(8,128)} fusion(bf16[1,2048,1536]{2,1,0:T(8,128)(2,1)} %all-gather.6.cloned.1.call-done, bf16[256,2048]{1,0:T(8,128)(2,1)} %copy-done.5, bf16[512,2048]{1,0:T(8,128)(2,1)} %copy-done.1), kind=kOutput, calls=%fused_computation.1 | convolution fusion | flops 4838129664 | bytes 14155776 | tf_op jit(solution)/shard_map/dot_general | solution.py:13
  287.4 42.7 %all-gather.4.cloned.1.call-done = bf16[2048,1536]{1,0:T(8,128)(2,1)} async-done(((bf16[512,1536]{1,0:T(8,128)(2,1)}), bf16[2048,1536]{1,0:T(8,128)(2,1)}) %all-gather.4.cloned.1.call-update) | async-done | bytes 6291472 | tf_op jit(solution)/shard_map/all_gather | solution.py:51
  330.1 12.5 %multiply_convert_fusion = bf16[768,1536]{1,0:T(8,128)(2,1)S(1)} fusion(f32[768,1536]{1,0:T(8,128)} %fusion.44, f32[768,1536]{1,0:T(8,128)} %fusion, bf16[2048,1536]{1,0:T(8,128)(2,1)} %all-gather.4.cloned.1.call-done, bf16[256,768]{1,0:T(8,128)(2,1)} %convolution_convert_fusion.4, bf16[512,768]{1,0:T(8,128)(2,1)} %get-tuple-element.7, ...), kind=kOutput, calls=%fused_computation.3 | convolution fusion | flops 4861722624 | bytes 23592960 | tf_op jit(solution)/shard_map/dot_general | solution.py:13
  342.6 0.7 convolution_convert_fusion.6
  343.3 0.6 fusion.13
  343.9 0.5 fusion.12
  344.9 11.0 %all_to_all.20 = f32[4,16,1408]{2,1,0:T(8,128)S(1)} all-to-all(f32[4,16,1408]{2,1,0:T(8,128)S(1)} %bitcast.84), channel_id=1, replica_groups=mesh['zh'=4,'y'=4,'c'=2,'zl'=2,'x'=4] {'x'}, dimensions={0} | all-to-all | bytes 720896 | tf_op jit(solution)/shard_map/all_to_all | solution.py:110
  356.0 11.1 %all_to_all.21 = bf16[8,16,1408]{2,1,0:T(8,128)(2,1)S(1)} all-to-all(bf16[8,16,1408]{2,1,0:T(8,128)(2,1)S(1)} %broadcast_in_dim.2), channel_id=1, replica_groups=mesh['zh'=4,'y'=4,'c'=2,'zl'=2,'x'=4] {'zl','x'}, dimensions={0} | all-to-all | bytes 720896 | tf_op jit(solution)/shard_map/all_to_all | solution.py:113
  367.1 0.7 slice_convert_fusion
  367.8 0.8 convert_bitcast_fusion
  (45 shorter events, 1.1 us)
Async XLA Ops:
  7.2 267.6 %copy-start = (bf16[2,16,1536]{2,1,0:T(8,128)(2,1)S(1)}, bf16[2,16,1536]{2,1,0:T(8,128)(2,1)}, u32[]{:S(2)}) copy-start(bf16[2,16,1536]{2,1,0:T(8,128)(2,1)} %param.11) | copy-start | bytes 294916
  16.0 68.9 %all-to-all-start = ((bf16[64,24,768]{2,1,0:T(8,128)(2,1)}), bf16[64,24,768]{2,1,0:T(8,128)(2,1)S(1)}, u32[]{:S(2)}, u32[]{:S(2)}) async-start(bf16[64,24,768]{2,1,0:T(8,128)(2,1)} %bitcast.80), calls=%async_computation | async-start | bytes 4718592 | tf_op jit(solution)/shard_map/all_to_all | solution.py:77
  28.1 249.5 %all-gather.6.cloned.1.call-start = ((), (), s32[]{:S(2)}) async-start(), calls=%async_computation.5 | async-start | bytes 7864320 | tf_op jit(solution)/shard_map/all_gather | solution.py:49
  28.2 5.4 %copy-start.3 = (bf16[128,4096]{1,0:T(8,128)(2,1)S(1)}, bf16[128,4096]{1,0:T(8,128)(2,1)}, u32[]{:S(2)}) copy-start(bf16[128,4096]{1,0:T(8,128)(2,1)} %param.6) | copy-start | bytes 3145732
  84.9 176.7 %copy-start.4 = (bf16[2,4096,16]{1,2,0:T(8,128)(2,1)S(1)}, bf16[2,4096,16]{1,2,0:T(8,128)(2,1)}, u32[]{:S(2)}) copy-start(bf16[2,4096,16]{1,2,0:T(8,128)(2,1)} %param.10) | copy-start | bytes 786436
  84.9 180.2 %all-to-all-start.1 = ((bf16[64,24,2048]{2,1,0:T(8,128)(2,1)}), bf16[64,24,2048]{2,1,0:T(8,128)(2,1)}, u32[]{:S(2)}, u32[]{:S(2)}) async-start(bf16[64,24,2048]{2,1,0:T(8,128)(2,1)} %bitcast.79), calls=%async_computation.1 | async-start | bytes 12582912 | tf_op jit(solution)/shard_map/all_to_all | solution.py:64
  90.7 239.4 %all-gather.4.cloned.1.call-start = ((), (), s32[]{:S(2)}) async-start(), calls=%async_computation.4 | async-start | bytes 7864320 | tf_op jit(solution)/shard_map/all_gather | solution.py:51
  90.8 170.7 %collective-permute-start = (bf16[512,1536]{1,0:T(8,128)(2,1)}, bf16[512,1536]{1,0:T(8,128)(2,1)}, u32[]{:S(2)}, u32[]{:S(2)}) collective-permute-start(bf16[512,1536]{1,0:T(8,128)(2,1)} %get-tuple-element.4), channel_id=1, source_target_pairs={{0,4},{4,0},{1,5},{5,1},{2,6},{6,2},{3,7},{7,3},{8,12},{12,8},{9,1... | collective-permute-start | bytes 4718600 | tf_op jit(solution)/shard_map/ppermute | solution.py:50
  267.4 3.0 copy-start.5
  270.4 3.3 copy-start.1
  273.8 1.0 copy-start.7
  330.1 13.2 %copy-start.2 = (bf16[512,2048]{1,0:T(8,128)(2,1)S(1)}, bf16[512,2048]{1,0:T(8,128)(2,1)}, u32[]{:S(2)}) copy-start(bf16[512,2048]{1,0:T(8,128)(2,1)} %copy-done.1) | copy-start | bytes 6291460
  330.1 13.2 %copy-start.6 = (bf16[256,2048]{1,0:T(8,128)(2,1)S(1)}, bf16[256,2048]{1,0:T(8,128)(2,1)}, u32[]{:S(2)}) copy-start(bf16[256,2048]{1,0:T(8,128)(2,1)} %copy-done.5) | copy-start | bytes 3145732
  342.6 1.3 copy-start.8
Sparse Core Ops, SparseCore 0:
  32.3 69.2 all-gather.5
  261.6 68.4 all-gather.3

commit v2 on v1

v2 whole, which is shorter than its diff:
```python
import jax
import jax.numpy as jnp
from jax import lax
from jax.sharding import Mesh, PartitionSpec as P

ADAPTER_SCALE = 2.0
EXPERT_AXES = ("zh", "y", "c")
DP_AXES = ("zl", "x")
PLANE = ("zh", "y", "c", "zl")


def dot(a, b, dims=((1,), (0,))):
    return lax.dot_general(a, b, (dims, ((), ())), preferred_element_type=jnp.float32)


def silu_slope(gate_preactivation):
    squash = jax.nn.sigmoid(gate_preactivation)
    return squash * (1.0 + gate_preactivation * (1.0 - squash))


def slot_targets(route, cap):
    rows, top = route.shape
    flat = route.T.reshape(rows * top)
    before = jnp.arange(rows * top)[:, None] > jnp.arange(rows * top)[None, :]
    same = flat[:, None] == flat[None, :]
    ranks = jnp.sum((same & before).astype(jnp.int32), axis=1)
    return (flat * cap + ranks).reshape(top, rows)


def send_places(experts, cap, swap):
    p = jnp.arange(experts * 24, dtype=jnp.int32)
    e, piece, r = p // 24, p % 24 // 8, p % 8
    rank = jnp.where(piece < 2, r, 8 + r % 4)
    half = jnp.where(piece < 2, piece, r // 4)
    if swap:
        half = jnp.where(e % 2 == 1, 1 - half, half)
    return e * cap + rank, half


RIGHT = [(i, (i + 1) % 4) for i in range(4)]
LEFT = [(i, (i - 1) % 4) for i in range(4)]


def first_hop(shard):
    return lax.ppermute(shard, "x", RIGHT), lax.ppermute(shard, "x", LEFT)


def second_hop(before, after):
    half = before.shape[0] // 2
    return lax.ppermute(before[:half], "x", RIGHT), lax.ppermute(after[half:], "x", LEFT)


def place_rows(buffer, shard, hop, opposite, x, base):
    rows = shard.shape[0]
    pieces = (
        (shard, x * rows),
        (hop[0], (x + 3) % 4 * rows),
        (hop[1], (x + 1) % 4 * rows),
        (opposite[0], (x + 2) % 4 * rows),
        (opposite[1], (x + 2) % 4 * rows + rows // 2),
    )
    for piece, start in pieces:
        buffer = lax.dynamic_update_slice(buffer, piece, (base + start, 0))
    return buffer


def local(tokens, route, gate_output_gradient, frozen_gate_weight, adapter_first, adapter_second):
    tok_rows, width = tokens.shape
    hidden = gate_output_gradient.shape[2]
    experts = 64
    cap = 12
    depth = 8
    zh, zl, x = lax.axis_index("zh"), lax.axis_index("zl"), lax.axis_index("x")
    half_width = width // 2

    lines = [
        lax.all_gather(tokens[:, h * half_width : (h + 1) * half_width], ("zh", "zl"), axis=0, tiled=True)
        for h in range(2)
    ]

    mine = lax.dynamic_index_in_dim(frozen_gate_weight, zl, 0, keepdims=False)
    other = lax.dynamic_index_in_dim(frozen_gate_weight, 1 - zl, 0, keepdims=False)
    got = lax.ppermute(other, "zl", [(0, 1), (1, 0)])
    near = first_hop(mine)
    line0, got, near = lax.optimization_barrier((lines[0], got, near))
    near_opposite = second_hop(*near)
    far = first_hop(got)
    line1, near_opposite, far = lax.optimization_barrier((lines[1], near_opposite, far))
    far_opposite = second_hop(*far)
    weight = jnp.zeros((width, hidden), jnp.bfloat16)
    weight = place_rows(weight, mine, near, near_opposite, x, zl * half_width)
    weight = place_rows(weight, got, far, far_opposite, x, (1 - zl) * half_width)
    first = lax.dynamic_index_in_dim(adapter_first, zl, 0, keepdims=False)
    second = lax.dynamic_index_in_dim(adapter_second, zl, 0, keepdims=False)

    target = slot_targets(route, cap)
    line_target = jnp.broadcast_to(target[None], (depth, 2, tok_rows))
    line_target = lax.all_to_all(line_target, ("zh", "zl"), split_axis=0, concat_axis=0, tiled=True)
    line_target = line_target.transpose(1, 0, 2).reshape(2, depth * tok_rows)
    row = jnp.arange(depth * depth * cap, dtype=jnp.int32)
    served = (zh * depth + row // (depth * cap)) * 2 + zl
    key = (served * cap + row % cap)[:, None]
    col = jnp.arange(depth * tok_rows, dtype=jnp.int32)
    same_block = (row // cap % depth)[:, None] == (col // tok_rows)[None, :]
    pick = same_block & ((line_target[0][None] == key) | (line_target[1][None] == key))
    pick = pick.astype(jnp.bfloat16)

    def spread(line):
        rows = dot(pick, line).astype(jnp.bfloat16).reshape(depth, depth * cap, half_width)
        rows = lax.all_to_all(rows, ("y", "c"), split_axis=0, concat_axis=0, tiled=True)
        return rows.reshape(depth * depth * cap, half_width)

    place, half = send_places(experts, cap, False)
    match = place[:, None] == target.reshape(1, 2 * tok_rows)
    pick_g = jnp.concatenate([match & (half == 0)[:, None], match & (half == 1)[:, None]], axis=1)
    half_hidden = hidden // 2
    parts = [
        gate_output_gradient[:, k, h * half_hidden : (h + 1) * half_hidden]
        for h in range(2)
        for k in range(2)
    ]
    send_g = dot(pick_g.astype(jnp.bfloat16), jnp.concatenate(parts, axis=0)).astype(jnp.bfloat16)
    send_g = send_g.reshape(experts, 24, half_hidden)

    x0 = spread(line0)
    send_g, line1 = lax.optimization_barrier((send_g, line1))
    x1 = spread(line1)
    recv_g = lax.all_to_all(send_g, PLANE, split_axis=0, concat_axis=0, tiled=True)
    recv_g = recv_g.reshape(experts * 24, half_hidden)

    block, rank = row // cap, row % cap
    source = block // 2 % 4 * 16 + block // 8 * 2 + block % 2
    q = jnp.arange(experts * 24, dtype=jnp.int32)

    def gather_half(h):
        at = source * 24 + jnp.where(rank < 8, 8 * h + rank, 16 + 4 * h + rank - 8)
        return dot((at[:, None] == q[None, :]).astype(jnp.bfloat16), recv_g)

    low = (dot(x0, first[:half_width]) + dot(x1, first[half_width:])).astype(jnp.bfloat16)
    frozen = dot(x0, weight[:half_width]) + dot(x1, weight[half_width:])
    preact = frozen + ADAPTER_SCALE * dot(low, second)
    rows_g = jnp.concatenate([gather_half(0), gather_half(1)], axis=1)
    slope = (rows_g * silu_slope(preact)).astype(jnp.bfloat16)
    back = dot(slope, second, ((1,), (1,))).astype(jnp.bfloat16)
    grads = ADAPTER_SCALE * jnp.concatenate(
        [
            dot(back, x0, ((0,), (0,))),
            dot(back, x1, ((0,), (0,))),
            dot(low, slope, ((0,), (0,))),
        ],
        axis=1,
    )

    rank = grads.shape[0]
    chunk = grads.shape[1] // 4
    parts = grads.reshape(rank, 4, chunk).transpose(1, 0, 2)
    parts = lax.all_to_all(parts, "x", split_axis=0, concat_axis=0, tiled=True)
    total = jnp.sum(parts, axis=0).astype(jnp.bfloat16)
    total = jnp.broadcast_to(total[None], (8, rank, chunk))
    total = lax.all_to_all(total, DP_AXES, split_axis=0, concat_axis=0, tiled=True)
    total = total.reshape(2, 4, rank, chunk).transpose(0, 2, 1, 3).reshape(2, rank, 4 * chunk)
    grad_a = total[:, :, :width].transpose(0, 2, 1).astype(jnp.float32)
    return grad_a, total[:, :, width:].astype(jnp.float32)


def solution(mesh):
    fine = Mesh(mesh.devices.reshape(4, 4, 2, 2, 4), EXPERT_AXES + DP_AXES)
    everyone = EXPERT_AXES + DP_AXES
    return jax.shard_map(
        local,
        mesh=fine,
        in_specs=(
            P(everyone, None),
            P(everyone, None),
            P(everyone, None, None),
            P(EXPERT_AXES, DP_AXES, None),
            P(EXPERT_AXES, None, None),
            P(EXPERT_AXES, None, None),
        ),
        out_specs=(P(EXPERT_AXES, None, None), P(EXPERT_AXES, None, None)),
        check_vma=False,
    )
```

time: 376 us -> 344 us (0.915)
  waiting for transfers between devices: 259 us -> 161 us
  local copies, waits for them, and re-layouts: 11.2 us -> 38.4 us
  matrix products: 43.6 us -> 65.5 us
  starting transfers between devices: 19.7 us -> 39.1 us
    ppermute x1, waiting for transfers between devices: 169 us -> 0.01 us  [local(): got = lax.ppermute(other, 'zl', [(0, 1), (1, 0)])]
    all_to_all x1 -> x3, waiting for transfers between devices: 0.01 us -> 104 us  [the longest x1 66.8 us: local(): lax.all_to_all(line_target, ('zh', 'zl'), split_axis=0, concat_axis=0, ti...]
    all_to_all x1, waiting for transfers between devices: 46.8 us -> 12.6 us  [local(): lax.all_to_all(send_g, PLANE, split_axis=0, concat_axis=0, tiled=True)]
    dot_general x15 -> x14, matrix products: 43.6 us -> 65.5 us  [dot(): lax.dot_general(a, b, (dims, ((), ())), preferred_element_type=jnp.float32)]
    dynamic_update_slice x0 -> x10, local copies, waits for them, and re-layouts: none -> 20.1 us  [place_rows(): buffer = lax.dynamic_update_slice(buffer, piece, (base + start, 0))]
    ppermute x0 -> x8, waiting for transfers between devices: none -> 15.9 us  [the longest x2 15.6 us: second_hop(): lax.ppermute(before[:half], 'x', RIGHT)]
    all_gather x2, waiting for transfers between devices: 42.7 us -> 27.6 us  [local(): lax.all_gather(tokens[:, h * half_width:(h + 1) * half_width], ('zh', 'zl...]
    ppermute x0 -> x8, starting transfers between devices: none -> 13.2 us  [the longest x4 6.55 us: first_hop(): return (lax.ppermute(shard, 'x', RIGHT), lax.ppermute(shard, 'x', LEFT))]
  transfers between devices with their start and end apart: 5 -> 15, of which waited for: 3 -> 7; matrix products, arithmetic and copies ran while one was open for 9% -> 21% of each run, Pallas kernels for 0% -> 0%
where the time goes in v2:
time: 344 us; the launch traced here: 342 us
  waiting for transfers between devices  161 us (47%)
  matrix products  65.5 us (19%)
  starting transfers between devices  39.1 us (11%)
  local copies, waits for them, and re-layouts  38.4 us (11%)
  blocking collectives  21.4 us (6%)
  between operations  14.3 us (4%)
    all_to_all x1, waiting for transfers between devices, local(): lax.all_to_all(line_target, ('zh', 'zl'), split_axis=0, concat_axis=0, ti...  66.8 us
    dot_general x14, matrix products, dot(): lax.dot_general(a, b, (dims, ((), ())), preferred_element_type=jnp.float32)  65.5 us
    all_to_all x2, waiting for transfers between devices, spread(): lax.all_to_all(rows, ('y', 'c'), split_axis=0, concat_axis=0, tiled=True)  37.1 us
    all_gather x2, waiting for transfers between devices, local(): lax.all_gather(tokens[:, h * half_width:(h + 1) * half_width], ('zh', 'zl...  27.6 us
    dynamic_update_slice x10, local copies, waits for them, and re-layouts, place_rows(): buffer = lax.dynamic_update_slice(buffer, piece, (base + start, 0))  20.1 us
    ppermute x2, waiting for transfers between devices, second_hop(): lax.ppermute(before[:half], 'x', RIGHT)  15.6 us
    all_to_all x1, waiting for transfers between devices, local(): lax.all_to_all(send_g, PLANE, split_axis=0, concat_axis=0, tiled=True)  12.6 us
    all_to_all x1, blocking collectives, local(): parts = lax.all_to_all(parts, 'x', split_axis=0, concat_axis=0, tiled=True)  11.2 us
  transfers between devices with their start and end apart: 15, of which 7 were waited for; matrix products, arithmetic and copies ran while one was open for 21% of the time, Pallas kernels for 0%

profile of v2, /device:TPU:8, one launch (start us, length us, event | category | flops | bytes accessed | tf_op | source)
XLA Modules:
  0.0 342.5 jit_solution(11891067372271791419)
XLA Ops:
  7.2 2.3 fusion.90
  10.3 5.3 %broadcast_in_dim.7 = bf16[4096,1536]{1,0:T(8,128)(2,1)} broadcast(bf16[]{:T(256)} %constant.218.clone.1), dimensions={} | broadcast | bytes 12582914 | tf_op jit(solution)/shard_map/broadcast_in_dim | solution.py:90
  20.8 2.7 dynamic-slice_bitcast_fusion.1
  26.1 7.6 %all-to-all-start.1 = ((s32[8,2,128]{2,1,0:T(2,128)}), s32[8,2,128]{2,1,0:T(2,128)S(1)}, u32[]{:S(2)}, u32[]{:S(2)}) async-start(s32[8,2,128]{2,1,0:T(2,128)} %broadcast_in_dim.6), calls=%async_computation.1 | async-start | bytes 16384 | tf_op jit(solution)/shard_map/all_to_all | solution.py:98
  33.7 66.8 %all-to-all-done.1 = s32[8,2,128]{2,1,0:T(2,128)S(1)} async-done(((s32[8,2,128]{2,1,0:T(2,128)}), s32[8,2,128]{2,1,0:T(2,128)S(1)}, u32[]{:S(2)}, u32[]{:S(2)}) %all-to-all-start.1) | async-done | bytes 8224 | tf_op jit(solution)/shard_map/all_to_all | solution.py:98
  100.6 8.2 %convolution_convert_fusion.1 = bf16[768,2048]{1,0:T(8,128)(2,1)} fusion(bf16[1024,2048]{1,0:T(8,128)(2,1)} %all-gather.5.cloned.1.call-done, s32[1024]{0:T(1024)S(1)} %bitcast.87, s32[1024]{0:T(1024)S(1)} %bitcast.85, s32[1024]{0:T(1024)S(1)} %add_select_fusion.5, s32[768]{0:T(1024)S(1)} %get-tuple-element.36, s32[768]{0:T(1024)S(1)} %get-tuple-element.37), kind=kOutput, calls=%fused_computation.11 | convolution fusion | flops 3226730496 | bytes 7358464 | tf_op jit(solution)/shard_map/dot_general | solution.py:13
  108.8 4.9 %all-to-all-start.2 = ((bf16[8,96,2048]{2,1,0:T(8,128)(2,1)}), bf16[8,96,2048]{2,1,0:T(8,128)(2,1)S(1)}, u32[]{:S(2)}, u32[]{:S(2)}) async-start(bf16[8,96,2048]{2,1,0:T(8,128)(2,1)} %bitcast.76), calls=%async_computation.2 | async-start | bytes 6291456 | tf_op jit(solution)/shard_map/all_to_all | solution.py:110
  114.2 2.9 collective-permute-start.6
  117.1 2.8 fusion.91
  122.0 3.2 collective-permute-start.4
  126.7 2.8 convolution_convert_fusion.2
  129.5 27.6 %all-gather.3.cloned.1.call-done = bf16[1024,2048]{1,0:T(8,128)(2,1)} async-done(((bf16[128,2048]{1,0:T(8,128)(2,1)}), bf16[1024,2048]{1,0:T(8,128)(2,1)}) %all-gather.3.cloned.1.call-update) | async-done | bytes 4194320 | tf_op jit(solution)/shard_map/all_gather | solution.py:77
  157.1 11.6 %collective-permute-done.3 = bf16[256,1536]{1,0:T(8,128)(2,1)} collective-permute-done((bf16[256,1536]{1,0:T(8,128)(2,1)}, bf16[256,1536]{1,0:T(8,128)(2,1)}, u32[]{:S(2)}, u32[]{:S(2)}) %collective-permute-start.3) | collective-permute-done | bytes 786464 | tf_op jit(solution)/shard_map/ppermute | solution.py:50
  168.7 7.2 %convolution_convert_fusion = bf16[768,2048]{1,0:T(8,128)(2,1)} fusion(bf16[1024,2048]{1,0:T(8,128)(2,1)} %all-gather.3.cloned.1.call-done, s32[1024]{0:T(1024)S(1)} %bitcast.88, s32[1024]{0:T(1024)S(1)} %bitcast.86, s32[1024]{0:T(1024)S(1)} %add_select_fusion.5, s32[768]{0:T(1024)S(1)} %get-tuple-element.36, s32[768]{0:T(1024)S(1)} %get-tuple-element.37), kind=kOutput, calls=%fused_computation.10 | convolution fusion | flops 3226730496 | bytes 7358464 | tf_op jit(solution)/shard_map/dot_general | solution.py:13
  175.9 4.8 %all-to-all-start.3 = ((bf16[8,96,2048]{2,1,0:T(8,128)(2,1)}), bf16[8,96,2048]{2,1,0:T(8,128)(2,1)}, u32[]{:S(2)}, u32[]{:S(2)}) async-start(bf16[8,96,2048]{2,1,0:T(8,128)(2,1)} %bitcast.75), calls=%async_computation.3 | async-start | bytes 6291456 | tf_op jit(solution)/shard_map/all_to_all | solution.py:110
  180.7 37.1 %all-to-all-done.3 = bf16[8,96,2048]{2,1,0:T(8,128)(2,1)} async-done(((bf16[8,96,2048]{2,1,0:T(8,128)(2,1)}), bf16[8,96,2048]{2,1,0:T(8,128)(2,1)}, u32[]{:S(2)}, u32[]{:S(2)}) %all-to-all-start.3) | async-done | bytes 3145760 | tf_op jit(solution)/shard_map/all_to_all | solution.py:110
  217.7 6.7 %all-to-all-start = ((bf16[64,24,768]{2,1,0:T(8,128)(2,1)}), bf16[64,24,768]{2,1,0:T(8,128)(2,1)}, u32[]{:S(2)}, u32[]{:S(2)}) async-start(bf16[64,24,768]{2,1,0:T(8,128)(2,1)} %bitcast.77), calls=%async_computation | async-start | bytes 4718592 | tf_op jit(solution)/shard_map/all_to_all | solution.py:128
  224.4 2.8 constant_dynamic-update-slice_fusion.8
  238.4 2.7 constant_dynamic-update-slice_fusion.4
  241.1 2.7 constant_dynamic-update-slice_fusion.3
  243.8 2.7 constant_dynamic-update-slice_fusion.2
  246.5 4.0 %collective-permute-done.7 = bf16[256,1536]{1,0:T(8,128)(2,1)S(1)} collective-permute-done((bf16[256,1536]{1,0:T(8,128)(2,1)S(1)}, bf16[256,1536]{1,0:T(8,128)(2,1)S(1)}, u32[]{:S(2)}, u32[]{:S(2)}) %collective-permute-start.7) | collective-permute-done | bytes 786464 | tf_op jit(solution)/shard_map/ppermute | solution.py:50
  253.6 3.2 fusion.14
  256.8 2.9 fusion.25
  259.8 8.8 %fusion = f32[768,1536]{0,1:T(8,128)} fusion(bf16[768,2048]{1,0:T(8,128)(2,1)} %bitcast.18, bf16[4096,1536]{1,0:T(8,128)(2,1)S(1)} %copy-done.2), kind=kOutput, calls=%fused_computation | convolution fusion | flops 4831838208 | bytes 14155776 | tf_op jit(solution)/shard_map/dot_general | solution.py:13
  268.6 12.6 %all-to-all-done = bf16[64,24,768]{2,1,0:T(8,128)(2,1)} async-done(((bf16[64,24,768]{2,1,0:T(8,128)(2,1)}), bf16[64,24,768]{2,1,0:T(8,128)(2,1)}, u32[]{:S(2)}, u32[]{:S(2)}) %all-to-all-start) | async-done | bytes 2359328 | tf_op jit(solution)/shard_map/all_to_all | solution.py:128
  281.1 5.3 %fusion.5 = f32[768,768]{0,1:T(8,128)} fusion(bf16[1536,768]{1,0:T(8,128)(2,1)} %bitcast.10, s32[768]{0:T(1024)S(1)} %get-tuple-element.38), kind=kOutput, calls=%fused_computation.8 | convolution fusion | flops 1813118976 | bytes 4721664 | tf_op jit(solution)/shard_map/dot_general | solution.py:13
  286.4 5.4 %fusion.6 = f32[768,768]{0,1:T(8,128)} fusion(bf16[1536,768]{1,0:T(8,128)(2,1)} %bitcast.10, s32[768]{0:T(1024)S(1)} %get-tuple-element.39), kind=kOutput, calls=%fused_computation.9 | convolution fusion | flops 1813118976 | bytes 4721664 | tf_op jit(solution)/shard_map/dot_general | solution.py:13
  291.8 14.7 %fusion.4 = bf16[768,1536]{0,1:T(8,128)(2,1)} fusion(f32[768,768]{0,1:T(8,128)} %fusion.6, f32[768,768]{0,1:T(8,128)} %fusion.5, f32[768,1536]{0,1:T(8,128)} %fusion.25, f32[768,1536]{0,1:T(8,128)} %fusion, bf16[768,2048]{1,0:T(8,128)(2,1)S(1)} %bitcast.73, bf16[4096,1536]{1,0:T(8,128)(2,1)} %constant_dynamic-update-slice_fusion), kind=kOutput, calls=%fused_computation.5 | convolution fusion | flops 4847173632 | bytes 25952256 | tf_op jit(solution)/shard_map/dot_general | solution.py:13
  309.2 2.6 fusion.94
  312.6 11.2 %all_to_all.30 = f32[4,16,1408]{2,1,0:T(8,128)S(1)} all-to-all(f32[4,16,1408]{2,1,0:T(8,128)S(1)} %bitcast.81), channel_id=1, replica_groups=mesh['zh'=4,'y'=4,'c'=2,'zl'=2,'x'=4] {'x'}, dimensions={0} | all-to-all | bytes 720896 | tf_op jit(solution)/shard_map/all_to_all | solution.py:157
  323.9 10.2 %all_to_all.31 = bf16[8,16,1408]{2,1,0:T(8,128)(2,1)S(1)} all-to-all(bf16[8,16,1408]{2,1,0:T(8,128)(2,1)S(1)} %broadcast_in_dim.8), channel_id=1, replica_groups=mesh['zh'=4,'y'=4,'c'=2,'zl'=2,'x'=4] {'zl','x'}, dimensions={0} | all-to-all | bytes 720896 | tf_op jit(solution)/shard_map/all_to_all | solution.py:160
  (78 shorter events, 31.8 us)
Async XLA Ops:
  7.2 245.5 %copy-start = (bf16[2,4096,16]{1,2,0:T(8,128)(2,1)S(1)}, bf16[2,4096,16]{1,2,0:T(8,128)(2,1)}, u32[]{:S(2)}) copy-start(bf16[2,4096,16]{1,2,0:T(8,128)(2,1)} %param.10) | copy-start | bytes 786436
  7.2 93.4 %all-gather.5.cloned.1.call-start = ((), (), s32[]{:S(2)}) async-start(), calls=%async_computation.7 | async-start | bytes 4718592 | tf_op jit(solution)/shard_map/all_gather | solution.py:77
  9.6 147.5 %all-gather.3.cloned.1.call-start = ((), (), s32[]{:S(2)}) async-start(), calls=%async_computation.6 | async-start | bytes 4718592 | tf_op jit(solution)/shard_map/all_gather | solution.py:77
  10.3 5.3 %copy-start.9 = (bf16[2,512,1536]{2,1,0:T(8,128)(2,1)S(1)}, bf16[2,512,1536]{2,1,0:T(8,128)(2,1)}, u32[]{:S(2)}) copy-start(bf16[2,512,1536]{2,1,0:T(8,128)(2,1)} %param.9) | copy-start | bytes 9437188
  15.7 9.7 %copy-start.11 = (s32[128,2]{0,1:T(2,128)S(1)}, s32[128,2]{0,1:T(2,128)}, u32[]{:S(2)}) copy-start(s32[128,2]{0,1:T(2,128)} %param.7) | copy-start | bytes 3076
  17.5 83.0 %collective-permute-start.1 = (bf16[512,1536]{1,0:T(8,128)(2,1)}, bf16[512,1536]{1,0:T(8,128)(2,1)S(1)}, u32[]{:S(2)}, u32[]{:S(2)}) collective-permute-start(bf16[512,1536]{1,0:T(8,128)(2,1)} %get-tuple-element.25), channel_id=1, source_target_pairs={{0,1},{1,2},{2,3},{3,0},{4,5},{5,6},{6,7},{7,4},{8,9},{9,10},{10,1... | collective-permute-start | bytes 4718600 | tf_op jit(solution)/shard_map/ppermute | solution.py:45
  19.0 81.5 %collective-permute-start.2 = (bf16[512,1536]{1,0:T(8,128)(2,1)}, bf16[512,1536]{1,0:T(8,128)(2,1)S(1)}, u32[]{:S(2)}, u32[]{:S(2)}) collective-permute-start(bf16[512,1536]{1,0:T(8,128)(2,1)} %get-tuple-element.25), channel_id=1, source_target_pairs={{0,3},{1,0},{2,1},{3,2},{4,7},{5,4},{6,5},{7,6},{8,11},{9,8},{10,9... | collective-permute-start | bytes 4718600 | tf_op jit(solution)/shard_map/ppermute | solution.py:45
  23.4 77.1 %collective-permute-start = (bf16[512,1536]{1,0:T(8,128)(2,1)}, bf16[512,1536]{1,0:T(8,128)(2,1)}, u32[]{:S(2)}, u32[]{:S(2)}) collective-permute-start(bf16[512,1536]{1,0:T(8,128)(2,1)} %dynamic-slice_bitcast_fusion.1), channel_id=1, source_target_pairs={{0,4},{4,0},{1,5},{5,1},{2,6},{6,2},{3,7},{7,3},{8,12},{12,8},{9,1... | collective-permute-start | bytes 4718600 | tf_op jit(solution)/shard_map/ppermute | solution.py:83
  26.1 74.4 %all-to-all-start.1 = ((s32[8,2,128]{2,1,0:T(2,128)}), s32[8,2,128]{2,1,0:T(2,128)S(1)}, u32[]{:S(2)}, u32[]{:S(2)}) async-start(s32[8,2,128]{2,1,0:T(2,128)} %broadcast_in_dim.6), calls=%async_computation.1 | async-start | bytes 16384 | tf_op jit(solution)/shard_map/all_to_all | solution.py:98
  100.5 8.3 %copy-start.4 = (bf16[512,1536]{1,0:T(8,128)(2,1)}, bf16[512,1536]{1,0:T(8,128)(2,1)S(1)}, u32[]{:S(2)}) copy-start(bf16[512,1536]{1,0:T(8,128)(2,1)S(1)} %collective-permute-done.1) | copy-start | bytes 4718596
  100.5 8.3 %copy-start.6 = (bf16[512,1536]{1,0:T(8,128)(2,1)}, bf16[512,1536]{1,0:T(8,128)(2,1)S(1)}, u32[]{:S(2)}) copy-start(bf16[512,1536]{1,0:T(8,128)(2,1)S(1)} %collective-permute-done.2) | copy-start | bytes 4718596
  108.8 67.0 %all-to-all-start.2 = ((bf16[8,96,2048]{2,1,0:T(8,128)(2,1)}), bf16[8,96,2048]{2,1,0:T(8,128)(2,1)S(1)}, u32[]{:S(2)}, u32[]{:S(2)}) async-start(bf16[8,96,2048]{2,1,0:T(8,128)(2,1)} %bitcast.76), calls=%async_computation.2 | async-start | bytes 6291456 | tf_op jit(solution)/shard_map/all_to_all | solution.py:110
  113.7 6.3 %copy-start.5 = (bf16[512,1536]{1,0:T(8,128)(2,1)S(1)}, bf16[512,1536]{1,0:T(8,128)(2,1)}, u32[]{:S(2)}) copy-start(bf16[512,1536]{1,0:T(8,128)(2,1)} %copy-done.4) | copy-start | bytes 4718596
  113.8 7.3 %copy-start.7 = (bf16[512,1536]{1,0:T(8,128)(2,1)S(1)}, bf16[512,1536]{1,0:T(8,128)(2,1)}, u32[]{:S(2)}) copy-start(bf16[512,1536]{1,0:T(8,128)(2,1)} %copy-done.6) | copy-start | bytes 4718596
  113.8 54.9 %collective-permute-start.5 = (bf16[512,1536]{1,0:T(8,128)(2,1)}, bf16[512,1536]{1,0:T(8,128)(2,1)}, u32[]{:S(2)}, u32[]{:S(2)}) collective-permute-start(bf16[512,1536]{1,0:T(8,128)(2,1)} %collective-permute-done), channel_id=1, source_target_pairs={{0,1},{1,2},{2,3},{3,0},{4,5},{5,6},{6,7},{7,4},{8,9},{9,10},{10,1... | collective-permute-start | bytes 4718600 | tf_op jit(solution)/shard_map/ppermute | solution.py:45
  114.2 54.5 %collective-permute-start.6 = (bf16[512,1536]{1,0:T(8,128)(2,1)}, bf16[512,1536]{1,0:T(8,128)(2,1)}, u32[]{:S(2)}, u32[]{:S(2)}) collective-permute-start(bf16[512,1536]{1,0:T(8,128)(2,1)} %collective-permute-done), channel_id=1, source_target_pairs={{0,3},{1,0},{2,1},{3,2},{4,7},{5,4},{6,5},{7,6},{8,11},{9,8},{10,9... | collective-permute-start | bytes 4718600 | tf_op jit(solution)/shard_map/ppermute | solution.py:45
  121.1 47.6 %collective-permute-start.3 = (bf16[256,1536]{1,0:T(8,128)(2,1)}, bf16[256,1536]{1,0:T(8,128)(2,1)}, u32[]{:S(2)}, u32[]{:S(2)}) collective-permute-start(bf16[256,1536]{1,0:T(8,128)(2,1)} %slice.68), channel_id=1, source_target_pairs={{0,1},{1,2},{2,3},{3,0},{4,5},{5,6},{6,7},{7,4},{8,9},{9,10},{10,1... | collective-permute-start | bytes 2359304 | tf_op jit(solution)/shard_map/ppermute | solution.py:50
  122.0 46.7 %collective-permute-start.4 = (bf16[256,1536]{1,0:T(8,128)(2,1)}, bf16[256,1536]{1,0:T(8,128)(2,1)}, u32[]{:S(2)}, u32[]{:S(2)}) collective-permute-start(bf16[256,1536]{1,0:T(8,128)(2,1)} %slice.69), channel_id=1, source_target_pairs={{0,3},{1,0},{2,1},{3,2},{4,7},{5,4},{6,5},{7,6},{8,11},{9,8},{10,9... | collective-permute-start | bytes 2359304 | tf_op jit(solution)/shard_map/ppermute | solution.py:50
  175.9 41.9 %all-to-all-start.3 = ((bf16[8,96,2048]{2,1,0:T(8,128)(2,1)}), bf16[8,96,2048]{2,1,0:T(8,128)(2,1)}, u32[]{:S(2)}, u32[]{:S(2)}) async-start(bf16[8,96,2048]{2,1,0:T(8,128)(2,1)} %bitcast.75), calls=%async_computation.3 | async-start | bytes 6291456 | tf_op jit(solution)/shard_map/all_to_all | solution.py:110
  217.7 63.4 %all-to-all-start = ((bf16[64,24,768]{2,1,0:T(8,128)(2,1)}), bf16[64,24,768]{2,1,0:T(8,128)(2,1)}, u32[]{:S(2)}, u32[]{:S(2)}) async-start(bf16[64,24,768]{2,1,0:T(8,128)(2,1)} %bitcast.77), calls=%async_computation | async-start | bytes 4718592 | tf_op jit(solution)/shard_map/all_to_all | solution.py:128
  224.4 2.9 copy-start.8
  229.7 20.9 %collective-permute-start.7 = (bf16[256,1536]{1,0:T(8,128)(2,1)S(1)}, bf16[256,1536]{1,0:T(8,128)(2,1)S(1)}, u32[]{:S(2)}, u32[]{:S(2)}) collective-permute-start(bf16[256,1536]{1,0:T(8,128)(2,1)S(1)} %slice.72), channel_id=1, source_target_pairs={{0,1},{1,2},{2,3},{3,0},{4,5},{5,6},{6,7},{7,4},{8,9},{9,10},{10,1... | collective-permute-start | bytes 2359304 | tf_op jit(solution)/shard_map/ppermute | solution.py:50
  232.4 19.4 %collective-permute-start.8 = (bf16[256,1536]{1,0:T(8,128)(2,1)S(1)}, bf16[256,1536]{1,0:T(8,128)(2,1)S(1)}, u32[]{:S(2)}, u32[]{:S(2)}) collective-permute-start(bf16[256,1536]{1,0:T(8,128)(2,1)S(1)} %slice.73), channel_id=1, source_target_pairs={{0,3},{1,0},{2,1},{3,2},{4,7},{5,4},{6,5},{7,6},{8,11},{9,8},{10,9... | collective-permute-start | bytes 2359304 | tf_op jit(solution)/shard_map/ppermute | solution.py:50
  251.8 5.1 %copy-start.10 = (bf16[2,16,1536]{2,1,0:T(8,128)(2,1)S(1)}, bf16[2,16,1536]{2,1,0:T(8,128)(2,1)}, u32[]{:S(2)}) copy-start(bf16[2,16,1536]{2,1,0:T(8,128)(2,1)} %param.11) | copy-start | bytes 294916
  252.7 7.1 %copy-start.2 = (bf16[4096,1536]{1,0:T(8,128)(2,1)S(1)}, bf16[4096,1536]{1,0:T(8,128)(2,1)}, u32[]{:S(2)}) copy-start(bf16[4096,1536]{1,0:T(8,128)(2,1)} %constant_dynamic-update-slice_fusion) | copy-start | bytes 37748740
  308.7 3.1 copy-start.3
  311.8 23.9 %copy-start.1 = (bf16[2,4096,16]{1,2,0:T(8,128)(2,1)S(1)}, bf16[2,4096,16]{1,2,0:T(8,128)(2,1)}, u32[]{:S(2)}) copy-start(bf16[2,4096,16]{1,2,0:T(8,128)(2,1)} %param.10) | copy-start | bytes 786436
Sparse Core Ops, SparseCore 0:
  9.8 89.5 all-gather.4
  101.8 55.2 all-gather.2

commit v3 on v2

v3 whole, which is shorter than its diff:
```python
import jax
import jax.numpy as jnp
from jax import lax
from jax.experimental import pallas as pl
from jax.experimental.pallas import tpu as pltpu
from jax.sharding import Mesh, PartitionSpec as P

ADAPTER_SCALE = 2.0
EXPERT_AXES = ("zh", "y", "c")
DP_AXES = ("zl", "x")
PLANE = ("zh", "y", "c", "zl")


def dot(a, b, dims=((1,), (0,))):
    return lax.dot_general(a, b, (dims, ((), ())), preferred_element_type=jnp.float32)


def silu_slope(gate_preactivation):
    squash = jax.nn.sigmoid(gate_preactivation)
    return squash * (1.0 + gate_preactivation * (1.0 - squash))


def slot_targets(route, cap):
    rows, top = route.shape
    flat = route.T.reshape(rows * top)
    before = jnp.arange(rows * top)[:, None] > jnp.arange(rows * top)[None, :]
    same = flat[:, None] == flat[None, :]
    ranks = jnp.sum((same & before).astype(jnp.int32), axis=1)
    return (flat * cap + ranks).reshape(top, rows)


def send_places(experts, cap, swap):
    p = jnp.arange(experts * 24, dtype=jnp.int32)
    e, piece, r = p // 24, p % 24 // 8, p % 8
    rank = jnp.where(piece < 2, r, 8 + r % 4)
    half = jnp.where(piece < 2, piece, r // 4)
    if swap:
        half = jnp.where(e % 2 == 1, 1 - half, half)
    return e * cap + rank, half


RIGHT = [(i, (i + 1) % 4) for i in range(4)]
LEFT = [(i, (i - 1) % 4) for i in range(4)]


def first_hop(shard):
    return lax.ppermute(shard, "x", RIGHT), lax.ppermute(shard, "x", LEFT)


def second_hop(before, after):
    half = before.shape[0] // 2
    return lax.ppermute(before[:half], "x", RIGHT), lax.ppermute(after[half:], "x", LEFT)


def weight_products(where_ref, x_ref, pieces):
    x, zl = where_ref[0], where_ref[1]
    width = x_ref.shape[1] // 8
    total = None
    for n, piece in enumerate(pieces):
        line = zl if n < 4 else 1 - zl
        at = pl.multiple_of((line * 4 + (x + (0, 3, 1, 2)[n % 4]) % 4) * width, width)
        product = dot(x_ref[:, pl.ds(at, width)], piece[...])
        total = product if total is None else total + product
    return total


def half_kernel(where_ref, x_ref, first_ref, *refs):
    frozen_ref, low_ref = refs[8:]
    frozen_ref[...] = weight_products(where_ref, x_ref, refs[:8])
    low_ref[...] = dot(x_ref[...], first_ref[...], ((1,), (1,)))


def final_kernel(where_ref, xa_ref, xb_ref, g0_ref, g1_ref, frozen_ref, lowa_ref, first_ref, second_ref, *refs):
    out_ref, frozen_acc, slope_acc, sums = refs[8:]
    step = pl.program_id(0)
    low = (lowa_ref[...] + dot(xb_ref[...], first_ref[...], ((1,), (1,)))).astype(jnp.bfloat16)
    frozen_acc[...] = frozen_ref[...] + weight_products(where_ref, xb_ref, refs[:8])
    half = g0_ref.shape[1]
    for h, g_ref in enumerate((g0_ref, g1_ref)):
        cols = slice(h * half, (h + 1) * half)
        preact = frozen_acc[:, cols] + ADAPTER_SCALE * dot(low, second_ref[:, cols])
        slope = g_ref[...].astype(jnp.float32) * silu_slope(preact)
        slope_acc[:, cols] = slope.astype(jnp.bfloat16)
    back = dot(slope_acc[...], second_ref[...], ((1,), (1,))).astype(jnp.bfloat16)

    @pl.when(step == 0)
    def _():
        sums[...] = jnp.zeros_like(sums)

    width = xa_ref.shape[1] // 8
    for h, x_ref in enumerate((xa_ref, xb_ref)):
        part = dot(back, x_ref[...], ((0,), (0,)))
        for n in range(8):
            at = (2 * n + h) * width
            sums[:, at : at + width] += part[:, n * width : (n + 1) * width]
    sums[:, 16 * width :] += dot(low, slope_acc[...], ((0,), (0,)))

    @pl.when(step == pl.num_programs(0) - 1)
    def _():
        chunk = out_ref.shape[2]
        for n in range(4):
            out_ref[n] = ADAPTER_SCALE * sums[:, n * chunk : (n + 1) * chunk]


ROW_BLOCK = 256


def row_spec(array):
    return pl.BlockSpec((ROW_BLOCK, array.shape[1]), lambda i, w: (i, 0))


def whole_spec(array):
    return pl.BlockSpec(array.shape, lambda i, w: (0, 0))


def piece_specs(pieces, h):
    specs = []
    for piece in pieces:
        at = h if piece.shape[0] == 512 else 0
        specs.append(pl.BlockSpec((256, piece.shape[1]), lambda i, w, at=at: (at, 0)))
    return specs


def half_products(where, x, first, pieces, h):
    rows, hidden, rank = x.shape[0], pieces[0].shape[1], first.shape[0]
    return pl.pallas_call(
        half_kernel,
        grid_spec=pltpu.PrefetchScalarGridSpec(
            num_scalar_prefetch=1,
            grid=(rows // ROW_BLOCK,),
            in_specs=[row_spec(x), whole_spec(first)] + piece_specs(pieces, h),
            out_specs=[
                pl.BlockSpec((ROW_BLOCK, hidden), lambda i, w: (i, 0)),
                pl.BlockSpec((ROW_BLOCK, rank), lambda i, w: (i, 0)),
            ],
        ),
        out_shape=[
            jax.ShapeDtypeStruct((rows, hidden), jnp.float32),
            jax.ShapeDtypeStruct((rows, rank), jnp.float32),
        ],
        name="half_products",
    )(where, x, first, *pieces)


def gradients(where, xa, xb, g0, g1, frozen, low, first, second, pieces, h):
    rows, hidden, rank = xa.shape[0], pieces[0].shape[1], first.shape[0]
    total = 2 * xa.shape[1] + hidden
    by_row = [row_spec(v) for v in (xa, xb, g0, g1, frozen, low)]
    return pl.pallas_call(
        final_kernel,
        grid_spec=pltpu.PrefetchScalarGridSpec(
            num_scalar_prefetch=1,
            grid=(rows // ROW_BLOCK,),
            in_specs=by_row + [whole_spec(first), whole_spec(second)] + piece_specs(pieces, h),
            out_specs=pl.BlockSpec((4, rank, total // 4), lambda i, w: (0, 0, 0)),
            scratch_shapes=[
                pltpu.VMEM((ROW_BLOCK, hidden), jnp.float32),
                pltpu.VMEM((ROW_BLOCK, hidden), jnp.bfloat16),
                pltpu.VMEM((rank, total), jnp.float32),
            ],
        ),
        out_shape=jax.ShapeDtypeStruct((4, rank, total // 4), jnp.float32),
        name="gradients",
    )(where, xa, xb, g0, g1, frozen, low, first, second, *pieces)


def split_kernel(tokens_ref, *out_refs):
    for h, out_ref in enumerate(out_refs):
        for n in range(out_ref.shape[1] // 256):
            at = (2 * n + h) * 256
            out_ref[:, n * 256 : (n + 1) * 256] = tokens_ref[:, at : at + 256]


def split_columns(tokens):
    shape = jax.ShapeDtypeStruct((tokens.shape[0], tokens.shape[1] // 2), tokens.dtype)
    return pl.pallas_call(split_kernel, out_shape=[shape, shape], name="split_columns")(tokens)


def local(tokens, route, gate_output_gradient, frozen_gate_weight, adapter_first, adapter_second):
    tok_rows, width = tokens.shape
    hidden = gate_output_gradient.shape[2]
    experts = 64
    cap = 12
    depth = 8
    zh, zl, x = lax.axis_index("zh"), lax.axis_index("zl"), lax.axis_index("x")
    half_width = width // 2

    lines = [
        lax.all_gather(part, ("zh", "zl"), axis=0, tiled=True) for part in split_columns(tokens)
    ]

    target = slot_targets(route, cap)
    line_target = jnp.broadcast_to(target[None], (depth, 2, tok_rows))
    line_target = lax.all_to_all(line_target, ("zh", "zl"), split_axis=0, concat_axis=0, tiled=True)

    mine = lax.dynamic_index_in_dim(frozen_gate_weight, zl, 0, keepdims=False)
    other = lax.dynamic_index_in_dim(frozen_gate_weight, 1 - zl, 0, keepdims=False)
    near = first_hop(mine)
    other, line_target = lax.optimization_barrier((other, line_target))
    got = lax.ppermute(other, "zl", [(0, 1), (1, 0)])

    place, half = send_places(experts, cap, False)
    match = place[:, None] == target.reshape(1, 2 * tok_rows)
    pick_g = jnp.concatenate([match & (half == 0)[:, None], match & (half == 1)[:, None]], axis=1)
    half_hidden = hidden // 2
    parts = [
        gate_output_gradient[:, k, h * half_hidden : (h + 1) * half_hidden]
        for h in range(2)
        for k in range(2)
    ]
    send_g = dot(pick_g.astype(jnp.bfloat16), jnp.concatenate(parts, axis=0)).astype(jnp.bfloat16)
    send_g = send_g.reshape(experts, 24, half_hidden)
    send_g, line_target = lax.optimization_barrier((send_g, line_target))
    recv_g = lax.all_to_all(send_g, PLANE, split_axis=0, concat_axis=0, tiled=True)

    line_target = line_target.transpose(1, 0, 2).reshape(2, depth * tok_rows)
    row = jnp.arange(depth * depth * cap, dtype=jnp.int32)
    served = (zh * depth + row // (depth * cap)) * 2 + zl
    key = (served * cap + row % cap)[:, None]
    col = jnp.arange(depth * tok_rows, dtype=jnp.int32)
    same_block = (row // cap % depth)[:, None] == (col // tok_rows)[None, :]
    pick = same_block & ((line_target[0][None] == key) | (line_target[1][None] == key))
    pick = pick.astype(jnp.bfloat16)

    def packed(line):
        return dot(pick, line).astype(jnp.bfloat16).reshape(depth, depth * cap, half_width)

    def spread(rows):
        rows = lax.all_to_all(rows, ("y", "c"), split_axis=0, concat_axis=0, tiled=True)
        return rows.reshape(depth * depth * cap, half_width)

    line0, got, near = lax.optimization_barrier((lines[0], got, near))
    near_opposite = second_hop(*near)
    far = first_hop(got)
    send_0, recv_g = lax.optimization_barrier((packed(line0), recv_g))
    xa = spread(send_0)
    line1, near_opposite, far = lax.optimization_barrier((lines[1], near_opposite, far))
    far_opposite = second_hop(*far)
    xb = spread(packed(line1))

    recv_g = recv_g.reshape(experts * 24, half_hidden)
    block, rank = row // cap, row % cap
    source = block // 2 % 4 * 16 + block // 8 * 2 + block % 2
    q = jnp.arange(experts * 24, dtype=jnp.int32)

    def gather_half(h):
        at = source * 24 + jnp.where(rank < 8, 8 * h + rank, 16 + 4 * h + rank - 8)
        return dot((at[:, None] == q[None, :]).astype(jnp.bfloat16), recv_g).astype(jnp.bfloat16)

    first = lax.dynamic_index_in_dim(adapter_first, zl, 0, keepdims=False)
    second = lax.dynamic_index_in_dim(adapter_second, zl, 0, keepdims=False)
    first = first.T
    first_a, first_b = (
        jnp.concatenate([first[:, at : at + 256] for at in range(256 * h, width, 512)], axis=1)
        for h in range(2)
    )
    where = jnp.stack([x, zl]).astype(jnp.int32)
    pieces = [
        [mine, *near, near_opposite[h], got, *far, far_opposite[h]]
        for h in range(2)
    ]
    frozen, low = half_products(where, xa, first_a, pieces[0], 0)
    parts = gradients(
        where, xa, xb, gather_half(0), gather_half(1), frozen, low, first_b, second, pieces[1], 1
    )

    rank, chunk = parts.shape[1:]
    parts = lax.all_to_all(parts, "x", split_axis=0, concat_axis=0, tiled=True)
    total = jnp.sum(parts, axis=0).astype(jnp.bfloat16)
    total = jnp.broadcast_to(total[None], (8, rank, chunk))
    total = lax.all_to_all(total, DP_AXES, split_axis=0, concat_axis=0, tiled=True)
    total = total.reshape(2, 4, rank, chunk).transpose(0, 2, 1, 3).reshape(2, rank, 4 * chunk)
    grad_a = total[:, :, :width].transpose(0, 2, 1).astype(jnp.float32)
    return grad_a, total[:, :, width:].astype(jnp.float32)


def solution(mesh):
    fine = Mesh(mesh.devices.reshape(4, 4, 2, 2, 4), EXPERT_AXES + DP_AXES)
    everyone = EXPERT_AXES + DP_AXES
    return jax.shard_map(
        local,
        mesh=fine,
        in_specs=(
            P(everyone, None),
            P(everyone, None),
            P(everyone, None, None),
            P(EXPERT_AXES, DP_AXES, None),
            P(EXPERT_AXES, None, None),
            P(EXPERT_AXES, None, None),
        ),
        out_specs=(P(EXPERT_AXES, None, None), P(EXPERT_AXES, None, None)),
        check_vma=False,
    )
```

time: 344 us -> 339 us (0.985)
  matrix products: 65.5 us -> 27.4 us
  Pallas kernels: 0 us -> 31.1 us
  local copies, waits for them, and re-layouts: 38.4 us -> 21.4 us
  waiting for transfers between devices: 161 us -> 171 us
  starting transfers between devices: 39.1 us -> 44.1 us
    ppermute x1, waiting for transfers between devices: 0.01 us -> 88.6 us  [local(): got = lax.ppermute(other, 'zl', [(0, 1), (1, 0)])]
    all_to_all x1, waiting for transfers between devices: 66.8 us -> 0.01 us  [local(): lax.all_to_all(line_target, ('zh', 'zl'), split_axis=0, concat_axis=0, ti...]
    dot_general x14 -> x5, matrix products: 65.5 us -> 27.4 us  [dot(): lax.dot_general(a, b, (dims, ((), ())), preferred_element_type=jnp.float32)]
    all_to_all x2, waiting for transfers between devices: 37.1 us -> 0.01 us  [spread(): lax.all_to_all(rows, ('y', 'c'), split_axis=0, concat_axis=0, tiled=True)]
    ppermute x2, waiting for transfers between devices: 15.6 us -> 49.1 us  [second_hop(): lax.ppermute(before[:half], 'x', RIGHT)]
    ppermute x4, waiting for transfers between devices: 0.01 us -> 33 us  [first_hop(): return (lax.ppermute(shard, 'x', RIGHT), lax.ppermute(shard, 'x', LEFT))]
    pallas_call x0 -> x3, Pallas kernels: none -> 31.1 us  [the longest x1 17.2 us: gradients(): pl.pallas_call(final_kernel, grid_spec=pltpu.PrefetchScalarGridSpec(num_s...]
    all_gather x2, waiting for transfers between devices: 27.6 us -> 0.01 us  [local(): lax.all_gather(part, ('zh', 'zl'), axis=0, tiled=True)]
  transfers between devices with their start and end apart: 15 -> 15, of which waited for: 7 -> 5; matrix products, arithmetic and copies ran while one was open for 21% -> 15% of each run, Pallas kernels for 0% -> 3%
where the time goes in v3:
time: 339 us; the launch traced here: 338 us
  waiting for transfers between devices  171 us (50%)
  starting transfers between devices  44.1 us (13%)
  Pallas kernels  31.1 us (9%)
  matrix products  27.4 us (8%)
  blocking collectives  22 us (6%)
  local copies, waits for them, and re-layouts  21.4 us (6%)
  between operations  14.2 us (4%)
  other arithmetic  6.01 us (2%)
    ppermute x1, waiting for transfers between devices, local(): got = lax.ppermute(other, 'zl', [(0, 1), (1, 0)])  88.6 us
    ppermute x2, waiting for transfers between devices, second_hop(): lax.ppermute(before[:half], 'x', RIGHT)  49.1 us
    ppermute x4, waiting for transfers between devices, first_hop(): return (lax.ppermute(shard, 'x', RIGHT), lax.ppermute(shard, 'x', LEFT))  33 us
    dot_general x5, matrix products, dot(): lax.dot_general(a, b, (dims, ((), ())), preferred_element_type=jnp.float32)  27.4 us
    pallas_call x1, Pallas kernels, gradients(): pl.pallas_call(final_kernel, grid_spec=pltpu.PrefetchScalarGridSpec(num_s...  17.2 us
    pallas_call x1, Pallas kernels, half_products(): pl.pallas_call(half_kernel, grid_spec=pltpu.PrefetchScalarGridSpec(num_sc...  11.5 us
    all_to_all x1, blocking collectives, local(): lax.all_to_all(total, DP_AXES, split_axis=0, concat_axis=0, tiled=True)  11.2 us
    all_to_all x1, starting transfers between devices, local(): lax.all_to_all(send_g, PLANE, split_axis=0, concat_axis=0, tiled=True)  11.1 us
  transfers between devices with their start and end apart: 15, of which 5 were waited for; matrix products, arithmetic and copies ran while one was open for 15% of the time, Pallas kernels for 3%

profile of v3, /device:TPU:8, one launch (start us, length us, event | category | flops | bytes accessed | tf_op | source)
XLA Modules:
  0.0 337.7 jit_solution(17760214368550451313)
XLA Ops:
  7.2 2.3 split_columns.1
  11.8 8.5 %all-to-all-start = ((s32[8,2,128]{2,1,0:T(2,128)}), s32[8,2,128]{2,1,0:T(2,128)S(1)}, u32[]{:S(2)}, u32[]{:S(2)}) async-start(s32[8,2,128]{2,1,0:T(2,128)} %broadcast_in_dim.4), calls=%async_computation | async-start | bytes 16384 | tf_op jit(solution)/shard_map/all_to_all | solution.py:194
  23.0 3.3 dynamic-slice_bitcast_fusion
  26.4 1.4 compare_and_fusion.1
  27.8 2.9 convolution_convert_fusion.2
  30.6 11.1 %all-to-all-start.1 = ((bf16[64,24,768]{2,1,0:T(8,128)(2,1)}), bf16[64,24,768]{2,1,0:T(8,128)(2,1)}, u32[]{:S(2)}, u32[]{:S(2)}) async-start(bf16[64,24,768]{2,1,0:T(8,128)(2,1)} %bitcast.53), calls=%async_computation.1 | async-start | bytes 4718592 | tf_op jit(solution)/shard_map/all_to_all | solution.py:214
  41.7 1.6 collective-permute-start.1
  43.3 1.7 collective-permute-start.2
  45.0 1.5 collective-permute-start
  46.6 32.9 %collective-permute-done.1.refs_1_ = bf16[512,1536]{1,0:T(8,128)(2,1)S(1)} collective-permute-done((bf16[512,1536]{1,0:T(8,128)(2,1)S(1)}, bf16[512,1536]{1,0:T(8,128)(2,1)S(1)}, u32[]{:S(2)}, u32[]{:S(2)}) %collective-permute-start.1) | collective-permute-done | bytes 1572896 | tf_op jit(solution)/shard_map/ppermute | solution.py:47
  79.5 88.6 %collective-permute-done.refs_4_ = bf16[512,1536]{1,0:T(8,128)(2,1)} collective-permute-done((bf16[512,1536]{1,0:T(8,128)(2,1)}, bf16[512,1536]{1,0:T(8,128)(2,1)}, u32[]{:S(2)}, u32[]{:S(2)}) %collective-permute-start) | collective-permute-done | bytes 1572896 | tf_op jit(solution)/shard_map/ppermute | solution.py:200
  168.2 7.3 %convolution_convert_fusion.1 = bf16[768,2048]{1,0:T(8,128)(2,1)} fusion(bf16[1024,2048]{1,0:T(8,128)(2,1)} %all-gather.3.cloned.1.call-done, s32[1024]{0:T(1024)S(1)} %bitcast.61, s32[1024]{0:T(1024)S(1)} %bitcast.59, s32[1024]{0:T(1024)S(1)} %add_select_fusion.9, s32[768]{0:T(1024)S(1)} %get-tuple-element.72, s32[768]{0:T(1024)S(1)} %get-tuple-element.73), kind=kOutput, calls=%fused_computation.5 | convolution fusion | flops 3226730496 | bytes 7358464 | tf_op jit(solution)/shard_map/dot_general | solution.py:15
  175.5 4.8 %all-to-all-start.2 = ((bf16[8,96,2048]{2,1,0:T(8,128)(2,1)}), bf16[8,96,2048]{2,1,0:T(8,128)(2,1)S(1)}, u32[]{:S(2)}, u32[]{:S(2)}) async-start(bf16[8,96,2048]{2,1,0:T(8,128)(2,1)} %bitcast.52), calls=%async_computation.2 | async-start | bytes 6291456 | tf_op jit(solution)/shard_map/all_to_all | solution.py:229
  180.3 1.5 collective-permute-start.5
  181.8 1.8 collective-permute-start.6
  183.6 2.1 slice.92
  186.0 2.1 slice.93
  188.0 3.0 collective-permute-start.4
  192.3 42.8 %collective-permute-done.3.refs_3_ = bf16[256,1536]{1,0:T(8,128)(2,1)} collective-permute-done((bf16[256,1536]{1,0:T(8,128)(2,1)}, bf16[256,1536]{1,0:T(8,128)(2,1)}, u32[]{:S(2)}, u32[]{:S(2)}) %collective-permute-start.3) | collective-permute-done | bytes 786464 | tf_op jit(solution)/shard_map/ppermute | solution.py:52
  235.1 7.5 %convolution_convert_fusion = bf16[768,2048]{1,0:T(8,128)(2,1)} fusion(bf16[1024,2048]{1,0:T(8,128)(2,1)} %all-gather.5.cloned.1.call-done, s32[1024]{0:T(1024)} %bitcast.62, s32[1024]{0:T(1024)} %bitcast.60, s32[1024]{0:T(1024)S(1)} %add_select_fusion.9, s32[768]{0:T(1024)S(1)} %get-tuple-element.72, s32[768]{0:T(1024)} %copy-done.7), kind=kOutput, calls=%fused_computation.4 | convolution fusion | flops 3226730496 | bytes 7358464 | tf_op jit(solution)/shard_map/dot_general | solution.py:15
  242.6 1.6 copy-done.1
  244.2 4.8 %all-to-all-start.3 = ((bf16[8,96,2048]{2,1,0:T(8,128)(2,1)}), bf16[8,96,2048]{2,1,0:T(8,128)(2,1)}, u32[]{:S(2)}, u32[]{:S(2)}) async-start(bf16[8,96,2048]{2,1,0:T(8,128)(2,1)} %bitcast.51), calls=%async_computation.3 | async-start | bytes 6291456 | tf_op jit(solution)/shard_map/all_to_all | solution.py:229
  253.2 1.4 dynamic-slice_bitcast_fusion.3.second_ref
  255.9 1.5 collective-permute-start.7
  258.5 2.1 collective-permute-start.8
  260.7 4.9 %fusion.8.g0_ref = bf16[768,768]{1,0:T(8,128)(2,1)} fusion(bf16[1536,768]{1,0:T(8,128)(2,1)} %bitcast.20, s32[768]{0:T(1024)S(1)} %fusion.53), kind=kOutput, calls=%fused_computation.18 | convolution fusion | flops 1813708800 | bytes 3542016 | tf_op jit(solution)/shard_map/dot_general | solution.py:15
  265.5 4.9 %fusion.7.g1_ref = bf16[768,768]{1,0:T(8,128)(2,1)} fusion(bf16[1536,768]{1,0:T(8,128)(2,1)} %bitcast.20, s32[768]{0:T(1024)S(1)} %fusion.54), kind=kOutput, calls=%fused_computation.17 | convolution fusion | flops 1813708800 | bytes 3542016 | tf_op jit(solution)/shard_map/dot_general | solution.py:15
  270.5 6.2 %collective-permute-done.7.refs_7_ = bf16[256,1536]{1,0:T(8,128)(2,1)S(1)} collective-permute-done((bf16[256,1536]{1,0:T(8,128)(2,1)S(1)}, bf16[256,1536]{1,0:T(8,128)(2,1)S(1)}, u32[]{:S(2)}, u32[]{:S(2)}) %collective-permute-start.7) | collective-permute-done | bytes 786464 | tf_op jit(solution)/shard_map/ppermute | solution.py:52
  277.6 11.5 %half_products.1 = (f32[768,1536]{1,0:T(8,128)}, f32[768,16]{1,0:T(8,128)}) custom-call(s32[2]{0:T(128)} %pad_add_fusion.where_ref, bf16[768,2048]{1,0:T(8,128)(2,1)} %bitcast.49, bf16[16,2048]{1,0:T(8,128)(2,1)} %get-tuple-element.47.first_ref, bf16[512,1536]{1,0:T(8,128)(2,1)} %copy-done.2, bf16[512,1536]{1,0:T(8,128)(2,1)} %copy-done.3, ...), custom_call_target="tpu_custom_call" | custom-call | tf_op jit(solution)/shard_map/half_products/pallas_call | solution.py:126
  290.0 17.2 %gradients.1 = f32[4,16,1408]{2,1,0:T(8,128)} custom-call(s32[2]{0:T(128)} %pad_add_fusion.where_ref, bf16[768,2048]{1,0:T(8,128)(2,1)} %bitcast.50, bf16[768,2048]{1,0:T(8,128)(2,1)} %bitcast.19.xb_ref, bf16[768,768]{1,0:T(8,128)(2,1)} %fusion.8.g0_ref, bf16[768,768]{1,0:T(8,128)(2,1)} %fusion.7.g1_ref, f32[768,1536]{1,0:T(8,128)} %get-tuple-element.37.frozen_ref, ...), custom_call_target="tpu_custom_call" | custom-call | tf_op jit(solution)/shard_map/gradients/pallas_call | solution.py:149
  307.3 10.8 %all_to_all.30 = f32[4,16,1408]{2,1,0:T(8,128)S(1)} all-to-all(f32[4,16,1408]{2,1,0:T(8,128)} %gradients.1), channel_id=1, replica_groups=mesh['zh'=4,'y'=4,'c'=2,'zl'=2,'x'=4] {'x'}, dimensions={0} | all-to-all | bytes 720896 | tf_op jit(solution)/shard_map/all_to_all | solution.py:268
  318.2 11.2 %all_to_all.31 = bf16[8,16,1408]{2,1,0:T(8,128)(2,1)S(1)} all-to-all(bf16[8,16,1408]{2,1,0:T(8,128)(2,1)S(1)} %broadcast_in_dim.5), channel_id=1, replica_groups=mesh['zh'=4,'y'=4,'c'=2,'zl'=2,'x'=4] {'zl','x'}, dimensions={0} | all-to-all | bytes 720896 | tf_op jit(solution)/shard_map/all_to_all | solution.py:271
  (66 shorter events, 16.7 us)
Async XLA Ops:
  7.2 184.5 %copy-start = (bf16[2,4096,16]{1,2,0:T(8,128)(2,1)S(1)}, bf16[2,4096,16]{1,2,0:T(8,128)(2,1)}, u32[]{:S(2)}) copy-start(bf16[2,4096,16]{1,2,0:T(8,128)(2,1)} %param.10) | copy-start | bytes 786436
  7.2 14.6 %copy-start.4 = (bf16[128,2,1536]{2,1,0:T(2,128)(2,1)S(1)}, bf16[128,2,1536]{2,1,0:T(2,128)(2,1)}, u32[]{:S(2)}) copy-start(bf16[128,2,1536]{2,1,0:T(2,128)(2,1)} %param.8) | copy-start | bytes 2359300
  7.2 161.0 %all-gather.3.cloned.1.call-start = ((), (), s32[]{:S(2)}) async-start(), calls=%async_computation.6 | async-start | bytes 4718592 | tf_op jit(solution)/shard_map/all_gather | solution.py:189
  11.8 18.8 %all-to-all-start = ((s32[8,2,128]{2,1,0:T(2,128)}), s32[8,2,128]{2,1,0:T(2,128)S(1)}, u32[]{:S(2)}, u32[]{:S(2)}) async-start(s32[8,2,128]{2,1,0:T(2,128)} %broadcast_in_dim.4), calls=%async_computation | async-start | bytes 16384 | tf_op jit(solution)/shard_map/all_to_all | solution.py:194
  20.3 172.0 %all-gather.5.cloned.1.call-start = ((), (), s32[]{:S(2)}) async-start(), calls=%async_computation.7 | async-start | bytes 4718592 | tf_op jit(solution)/shard_map/all_gather | solution.py:189
  26.4 16.9 %copy-start.2 = (bf16[512,1536]{1,0:T(8,128)(2,1)}, bf16[512,1536]{1,0:T(8,128)(2,1)S(1)}, u32[]{:S(2)}) copy-start(bf16[512,1536]{1,0:T(8,128)(2,1)S(1)} %get-tuple-element.40.refs_0_) | copy-start | bytes 4718596
  30.6 144.8 %all-to-all-start.1 = ((bf16[64,24,768]{2,1,0:T(8,128)(2,1)}), bf16[64,24,768]{2,1,0:T(8,128)(2,1)}, u32[]{:S(2)}, u32[]{:S(2)}) async-start(bf16[64,24,768]{2,1,0:T(8,128)(2,1)} %bitcast.53), calls=%async_computation.1 | async-start | bytes 4718592 | tf_op jit(solution)/shard_map/all_to_all | solution.py:214
  41.7 37.7 %collective-permute-start.1 = (bf16[512,1536]{1,0:T(8,128)(2,1)S(1)}, bf16[512,1536]{1,0:T(8,128)(2,1)S(1)}, u32[]{:S(2)}, u32[]{:S(2)}) collective-permute-start(bf16[512,1536]{1,0:T(8,128)(2,1)S(1)} %get-tuple-element.40.refs_0_), channel_id=1, source_target_pairs={{0,1},{1,2},{2,3},{3,0},{4,5},{5,6},{6,7},{7,4},{8,9},{9,10},{10,1... | collective-permute-start | bytes 4718600 | tf_op jit(solution)/shard_map/ppermute | solution.py:47
  43.3 36.2 %collective-permute-start.2 = (bf16[512,1536]{1,0:T(8,128)(2,1)S(1)}, bf16[512,1536]{1,0:T(8,128)(2,1)}, u32[]{:S(2)}, u32[]{:S(2)}) collective-permute-start(bf16[512,1536]{1,0:T(8,128)(2,1)S(1)} %get-tuple-element.40.refs_0_), channel_id=1, source_target_pairs={{0,3},{1,0},{2,1},{3,2},{4,7},{5,4},{6,5},{7,6},{8,11},{9,8},{10,9... | collective-permute-start | bytes 4718600 | tf_op jit(solution)/shard_map/ppermute | solution.py:47
  45.0 123.1 %collective-permute-start = (bf16[512,1536]{1,0:T(8,128)(2,1)}, bf16[512,1536]{1,0:T(8,128)(2,1)}, u32[]{:S(2)}, u32[]{:S(2)}) collective-permute-start(bf16[512,1536]{1,0:T(8,128)(2,1)} %get-tuple-element.24), channel_id=1, source_target_pairs={{0,4},{4,0},{1,5},{5,1},{2,6},{6,2},{3,7},{7,3},{8,12},{12,8},{9,1... | collective-permute-start | bytes 4718600 | tf_op jit(solution)/shard_map/ppermute | solution.py:200
  46.5 128.9 %copy-start.7 = (s32[768]{0:T(1024)}, s32[768]{0:T(1024)S(1)}, u32[]{:S(2)}) copy-start(s32[768]{0:T(1024)S(1)} %get-tuple-element.73) | copy-start | bytes 9220
  46.5 128.9 %copy-start.8 = (s32[1,8,128]{2,0,1:T(1,128)}, s32[1,8,128]{2,0,1:T(1,128)S(1)}, u32[]{:S(2)}) copy-start(s32[1,8,128]{2,0,1:T(1,128)S(1)} %get-tuple-element.64) | copy-start | bytes 12292
  46.5 128.9 %copy-start.9 = (s32[1,8,128]{2,0,1:T(1,128)}, s32[1,8,128]{2,0,1:T(1,128)S(1)}, u32[]{:S(2)}) copy-start(s32[1,8,128]{2,0,1:T(1,128)S(1)} %get-tuple-element.65) | copy-start | bytes 12292
  79.4 96.0 %copy-start.3 = (bf16[512,1536]{1,0:T(8,128)(2,1)}, bf16[512,1536]{1,0:T(8,128)(2,1)S(1)}, u32[]{:S(2)}) copy-start(bf16[512,1536]{1,0:T(8,128)(2,1)S(1)} %collective-permute-done.1.refs_1_) | copy-start | bytes 4718596
  175.5 67.1 %all-to-all-start.2 = ((bf16[8,96,2048]{2,1,0:T(8,128)(2,1)}), bf16[8,96,2048]{2,1,0:T(8,128)(2,1)S(1)}, u32[]{:S(2)}, u32[]{:S(2)}) async-start(bf16[8,96,2048]{2,1,0:T(8,128)(2,1)} %bitcast.52), calls=%async_computation.2 | async-start | bytes 6291456 | tf_op jit(solution)/shard_map/all_to_all | solution.py:229
  180.3 54.8 %collective-permute-start.5 = (bf16[512,1536]{1,0:T(8,128)(2,1)}, bf16[512,1536]{1,0:T(8,128)(2,1)}, u32[]{:S(2)}, u32[]{:S(2)}) collective-permute-start(bf16[512,1536]{1,0:T(8,128)(2,1)} %collective-permute-done.refs_4_), channel_id=1, source_target_pairs={{0,1},{1,2},{2,3},{3,0},{4,5},{5,6},{6,7},{7,4},{8,9},{9,10},{10,1... | collective-permute-start | bytes 4718600 | tf_op jit(solution)/shard_map/ppermute | solution.py:47
  181.8 53.3 %collective-permute-start.6 = (bf16[512,1536]{1,0:T(8,128)(2,1)}, bf16[512,1536]{1,0:T(8,128)(2,1)}, u32[]{:S(2)}, u32[]{:S(2)}) collective-permute-start(bf16[512,1536]{1,0:T(8,128)(2,1)} %collective-permute-done.refs_4_), channel_id=1, source_target_pairs={{0,3},{1,0},{2,1},{3,2},{4,7},{5,4},{6,5},{7,6},{8,11},{9,8},{10,9... | collective-permute-start | bytes 4718600 | tf_op jit(solution)/shard_map/ppermute | solution.py:47
  185.7 49.4 %collective-permute-start.3 = (bf16[256,1536]{1,0:T(8,128)(2,1)}, bf16[256,1536]{1,0:T(8,128)(2,1)}, u32[]{:S(2)}, u32[]{:S(2)}) collective-permute-start(bf16[256,1536]{1,0:T(8,128)(2,1)} %slice.92), channel_id=1, source_target_pairs={{0,1},{1,2},{2,3},{3,0},{4,5},{5,6},{6,7},{7,4},{8,9},{9,10},{10,1... | collective-permute-start | bytes 2359304 | tf_op jit(solution)/shard_map/ppermute | solution.py:52
  188.0 47.1 %collective-permute-start.4 = (bf16[256,1536]{1,0:T(8,128)(2,1)}, bf16[256,1536]{1,0:T(8,128)(2,1)}, u32[]{:S(2)}, u32[]{:S(2)}) collective-permute-start(bf16[256,1536]{1,0:T(8,128)(2,1)} %slice.93), channel_id=1, source_target_pairs={{0,3},{1,0},{2,1},{3,2},{4,7},{5,4},{6,5},{7,6},{8,11},{9,8},{10,9... | collective-permute-start | bytes 2359304 | tf_op jit(solution)/shard_map/ppermute | solution.py:52
  242.6 1.6 copy-start.1
  244.2 44.9 %all-to-all-start.3 = ((bf16[8,96,2048]{2,1,0:T(8,128)(2,1)}), bf16[8,96,2048]{2,1,0:T(8,128)(2,1)}, u32[]{:S(2)}, u32[]{:S(2)}) async-start(bf16[8,96,2048]{2,1,0:T(8,128)(2,1)} %bitcast.51), calls=%async_computation.3 | async-start | bytes 6291456 | tf_op jit(solution)/shard_map/all_to_all | solution.py:229
  255.9 20.9 %collective-permute-start.7 = (bf16[256,1536]{1,0:T(8,128)(2,1)S(1)}, bf16[256,1536]{1,0:T(8,128)(2,1)S(1)}, u32[]{:S(2)}, u32[]{:S(2)}) collective-permute-start(bf16[256,1536]{1,0:T(8,128)(2,1)S(1)} %slice.102), channel_id=1, source_target_pairs={{0,1},{1,2},{2,3},{3,0},{4,5},{5,6},{6,7},{7,4},{8,9},{9,10},{10,1... | collective-permute-start | bytes 2359304 | tf_op jit(solution)/shard_map/ppermute | solution.py:52
  258.5 30.6 %collective-permute-start.8 = (bf16[256,1536]{1,0:T(8,128)(2,1)S(1)}, bf16[256,1536]{1,0:T(8,128)(2,1)S(1)}, u32[]{:S(2)}, u32[]{:S(2)}) collective-permute-start(bf16[256,1536]{1,0:T(8,128)(2,1)S(1)} %slice.111), channel_id=1, source_target_pairs={{0,3},{1,0},{2,1},{3,2},{4,7},{5,4},{6,5},{7,6},{8,11},{9,8},{10,9... | collective-permute-start | bytes 2359304 | tf_op jit(solution)/shard_map/ppermute | solution.py:52
  276.7 0.9 copy-start.6
  289.1 0.9 copy-start.5
Sparse Core Ops, SparseCore 0:
  10.4 104.8 all-gather.2
  117.0 72.8 all-gather.4

commit v4 on v3

--- a/solution.py
+++ b/solution.py
@@ -229,12 +229,12 @@
         rows = lax.all_to_all(rows, ("y", "c"), split_axis=0, concat_axis=0, tiled=True)
         return rows.reshape(depth * depth * cap, half_width)
 
-    line0, got, near = lax.optimization_barrier((lines[0], got, near))
     near_opposite = second_hop(*near)
+    line0, near_opposite = lax.optimization_barrier((lines[0], near_opposite))
+    send_0, recv_g, got = lax.optimization_barrier((packed(line0), recv_g, got))
     far = first_hop(got)
-    send_0, recv_g = lax.optimization_barrier((packed(line0), recv_g))
     xa = spread(send_0)
-    line1, near_opposite, far = lax.optimization_barrier((lines[1], near_opposite, far))
+    line1, far = lax.optimization_barrier((lines[1], far))
     far_opposite = second_hop(*far)
     xb = spread(packed(line1))
 
@@ -277,8 +277,12 @@
 def solution(mesh):
     fine = Mesh(mesh.devices.reshape(4, 4, 2, 2, 4), EXPERT_AXES + DP_AXES)
     everyone = EXPERT_AXES + DP_AXES
-    return jax.shard_map(
-        local,
+
+    def step(*args):
+        return local(*args)
+
+    step = jax.shard_map(
+        step,
         mesh=fine,
         in_specs=(
             P(everyone, None),
@@ -291,3 +295,4 @@
         out_specs=(P(EXPERT_AXES, None, None), P(EXPERT_AXES, None, None)),
         check_vma=False,
     )
+    return step

time: 339 us -> 315 us (0.929)
  waiting for transfers between devices: 171 us -> 149 us
    ppermute x1, waiting for transfers between devices: 88.6 us -> 45.5 us  [local(): got = lax.ppermute(other, 'zl', [(0, 1), (1, 0)])]
    ppermute x2, waiting for transfers between devices: 49.1 us -> 22.3 us  [second_hop(): lax.ppermute(before[:half], 'x', RIGHT)]
    all_gather x2, waiting for transfers between devices: 0.01 us -> 25.6 us  [local(): lax.all_gather(part, ('zh', 'zl'), axis=0, tiled=True)]
    ppermute x4, waiting for transfers between devices: 33 us -> 55 us  [first_hop(): return (lax.ppermute(shard, 'x', RIGHT), lax.ppermute(shard, 'x', LEFT))]
    unnamed x27 -> x33, local copies, waits for them, and re-layouts: 7.67 us -> 10.1 us
  transfers between devices with their start and end apart: 15 -> 15, of which waited for: 5 -> 8; matrix products, arithmetic and copies ran while one was open for 15% -> 15% of each run, Pallas kernels for 3% -> 4%
where the time goes in v4:
time: 315 us; the launch traced here: 314 us
  waiting for transfers between devices  149 us (47%)
  starting transfers between devices  43.7 us (14%)
  Pallas kernels  30.9 us (10%)
  matrix products  27.4 us (9%)
  blocking collectives  22 us (7%)
  local copies, waits for them, and re-layouts  20.8 us (7%)
  between operations  14.3 us (5%)
  other arithmetic  6.01 us (2%)
    ppermute x4, waiting for transfers between devices, first_hop(): return (lax.ppermute(shard, 'x', RIGHT), lax.ppermute(shard, 'x', LEFT))  55 us
    ppermute x1, waiting for transfers between devices, local(): got = lax.ppermute(other, 'zl', [(0, 1), (1, 0)])  45.5 us
    dot_general x5, matrix products, dot(): lax.dot_general(a, b, (dims, ((), ())), preferred_element_type=jnp.float32)  27.4 us
    all_gather x2, waiting for transfers between devices, local(): lax.all_gather(part, ('zh', 'zl'), axis=0, tiled=True)  25.6 us
    ppermute x2, waiting for transfers between devices, second_hop(): lax.ppermute(before[:half], 'x', RIGHT)  22.3 us
    pallas_call x1, Pallas kernels, gradients(): pl.pallas_call(final_kernel, grid_spec=pltpu.PrefetchScalarGridSpec(num_s...  17.2 us
    pallas_call x1, Pallas kernels, half_products(): pl.pallas_call(half_kernel, grid_spec=pltpu.PrefetchScalarGridSpec(num_sc...  11.3 us
    all_to_all x1, blocking collectives, local(): lax.all_to_all(total, DP_AXES, split_axis=0, concat_axis=0, tiled=True)  11.2 us
  transfers between devices with their start and end apart: 15, of which 8 were waited for; matrix products, arithmetic and copies ran while one was open for 15% of the time, Pallas kernels for 4%

profile of v4, /device:TPU:8, one launch (start us, length us, event | category | flops | bytes accessed | tf_op | source)
XLA Modules:
  0.0 314.5 jit_solution(8604831932464726857)
XLA Ops:
  7.2 2.3 split_columns.1
  11.8 8.5 %all-to-all-start = ((s32[8,2,128]{2,1,0:T(2,128)}), s32[8,2,128]{2,1,0:T(2,128)S(1)}, u32[]{:S(2)}, u32[]{:S(2)}) async-start(s32[8,2,128]{2,1,0:T(2,128)} %broadcast_in_dim.4), calls=%async_computation | async-start | bytes 16384 | tf_op jit(solution)/shard_map/all_to_all | solution.py:194
  23.0 3.3 %dynamic-slice_bitcast_fusion.1 = (bf16[512,1536]{1,0:T(8,128)(2,1)}, bf16[512,1536]{1,0:T(8,128)(2,1)S(1)}) fusion(bf16[2,512,1536]{2,1,0:T(8,128)(2,1)} %param.9, s32[]{:T(128)S(6)} %select_n.256, s32[]{:T(128)S(6)} %select_n.259), kind=kLoop, calls=%fused_computation.16 | loop fusion | bytes 6291464 | tf_op jit(solution)/shard_map/jit(dynamic_index_in_dim)/squeeze | solution.py:197
  27.7 2.9 convolution_convert_fusion.2
  30.6 11.1 %all-to-all-start.1 = ((bf16[64,24,768]{2,1,0:T(8,128)(2,1)}), bf16[64,24,768]{2,1,0:T(8,128)(2,1)}, u32[]{:S(2)}, u32[]{:S(2)}) async-start(bf16[64,24,768]{2,1,0:T(8,128)(2,1)} %bitcast.53), calls=%async_computation.1 | async-start | bytes 4718592 | tf_op jit(solution)/shard_map/all_to_all | solution.py:214
  41.7 1.6 collective-permute-start
  43.3 1.7 collective-permute-start.2
  45.0 1.5 collective-permute-start.4
  46.5 32.9 %collective-permute-done.refs_1_ = bf16[512,1536]{1,0:T(8,128)(2,1)S(1)} collective-permute-done((bf16[512,1536]{1,0:T(8,128)(2,1)S(1)}, bf16[512,1536]{1,0:T(8,128)(2,1)S(1)}, u32[]{:S(2)}, u32[]{:S(2)}) %collective-permute-start) | collective-permute-done | bytes 1572896 | tf_op jit(solution)/shard_map/ppermute | solution.py:47
  82.1 2.8 collective-permute-start.3
  84.9 15.9 %collective-permute-done.1.refs_3_ = bf16[256,1536]{1,0:T(8,128)(2,1)} collective-permute-done((bf16[256,1536]{1,0:T(8,128)(2,1)}, bf16[256,1536]{1,0:T(8,128)(2,1)}, u32[]{:S(2)}, u32[]{:S(2)}) %collective-permute-start.1) | collective-permute-done | bytes 786464 | tf_op jit(solution)/shard_map/ppermute | solution.py:52
  100.9 14.3 %all-gather.3.cloned.1.call-done = bf16[1024,2048]{1,0:T(8,128)(2,1)} async-done(((bf16[128,2048]{1,0:T(8,128)(2,1)}), bf16[1024,2048]{1,0:T(8,128)(2,1)}) %all-gather.3.cloned.1.call-update) | async-done | bytes 4194320 | tf_op jit(solution)/shard_map/all_gather | solution.py:189
  115.2 7.2 %convolution_convert_fusion.1 = bf16[768,2048]{1,0:T(8,128)(2,1)} fusion(bf16[1024,2048]{1,0:T(8,128)(2,1)} %all-gather.3.cloned.1.call-done, s32[1024]{0:T(1024)S(1)} %bitcast.61, s32[1024]{0:T(1024)S(1)} %bitcast.59, s32[1024]{0:T(1024)S(1)} %add_select_fusion.9, s32[768]{0:T(1024)S(1)} %get-tuple-element.68, s32[768]{0:T(1024)S(1)} %get-tuple-element.69), kind=kOutput, calls=%fused_computation.5 | convolution fusion | flops 3226730496 | bytes 7358464 | tf_op jit(solution)/shard_map/dot_general | solution.py:15
  122.5 45.5 %collective-permute-done.4.refs_4_ = bf16[512,1536]{1,0:T(8,128)(2,1)S(1)} collective-permute-done((bf16[512,1536]{1,0:T(8,128)(2,1)}, bf16[512,1536]{1,0:T(8,128)(2,1)S(1)}, u32[]{:S(2)}, u32[]{:S(2)}) %collective-permute-start.4) | collective-permute-done | bytes 1572896 | tf_op jit(solution)/shard_map/ppermute | solution.py:200
  169.2 4.8 %all-to-all-start.2 = ((bf16[8,96,2048]{2,1,0:T(8,128)(2,1)}), bf16[8,96,2048]{2,1,0:T(8,128)(2,1)S(1)}, u32[]{:S(2)}, u32[]{:S(2)}) async-start(bf16[8,96,2048]{2,1,0:T(8,128)(2,1)} %bitcast.52), calls=%async_computation.2 | async-start | bytes 6291456 | tf_op jit(solution)/shard_map/all_to_all | solution.py:229
  174.1 1.5 collective-permute-start.5
  175.5 1.8 collective-permute-start.6
  178.7 11.3 %all-gather.5.cloned.1.call-done = bf16[1024,2048]{1,0:T(8,128)(2,1)} async-done(((bf16[128,2048]{1,0:T(8,128)(2,1)}), bf16[1024,2048]{1,0:T(8,128)(2,1)}) %all-gather.5.cloned.1.call-update) | async-done | bytes 4194320 | tf_op jit(solution)/shard_map/all_gather | solution.py:189
  190.0 22.0 %collective-permute-done.5.refs_5_ = bf16[512,1536]{1,0:T(8,128)(2,1)} collective-permute-done((bf16[512,1536]{1,0:T(8,128)(2,1)}, bf16[512,1536]{1,0:T(8,128)(2,1)}, u32[]{:S(2)}, u32[]{:S(2)}) %collective-permute-start.5) | collective-permute-done | bytes 1572896 | tf_op jit(solution)/shard_map/ppermute | solution.py:47
  212.0 7.4 %convolution_convert_fusion = bf16[768,2048]{1,0:T(8,128)(2,1)} fusion(bf16[1024,2048]{1,0:T(8,128)(2,1)} %all-gather.5.cloned.1.call-done, s32[1024]{0:T(1024)} %bitcast.62, s32[1024]{0:T(1024)} %bitcast.60, s32[1024]{0:T(1024)S(1)} %add_select_fusion.9, s32[768]{0:T(1024)S(1)} %get-tuple-element.68, s32[768]{0:T(1024)} %copy-done.10), kind=kOutput, calls=%fused_computation.4 | convolution fusion | flops 3226730496 | bytes 7358464 | tf_op jit(solution)/shard_map/dot_general | solution.py:15
  219.5 1.6 copy-done.1
  221.1 4.8 %all-to-all-start.3 = ((bf16[8,96,2048]{2,1,0:T(8,128)(2,1)}), bf16[8,96,2048]{2,1,0:T(8,128)(2,1)}, u32[]{:S(2)}, u32[]{:S(2)}) async-start(bf16[8,96,2048]{2,1,0:T(8,128)(2,1)} %bitcast.51), calls=%async_computation.3 | async-start | bytes 6291456 | tf_op jit(solution)/shard_map/all_to_all | solution.py:229
  230.1 1.4 dynamic-slice_bitcast_fusion.3.second_ref
  232.7 1.5 collective-permute-start.7
  235.4 1.9 collective-permute-start.8
  237.3 4.9 %fusion.8.g0_ref = bf16[768,768]{1,0:T(8,128)(2,1)} fusion(bf16[1536,768]{1,0:T(8,128)(2,1)} %bitcast.20, s32[768]{0:T(1024)S(1)} %fusion.53), kind=kOutput, calls=%fused_computation.18 | convolution fusion | flops 1813708800 | bytes 3542016 | tf_op jit(solution)/shard_map/dot_general | solution.py:15
  242.2 4.9 %fusion.7.g1_ref = bf16[768,768]{1,0:T(8,128)(2,1)} fusion(bf16[1536,768]{1,0:T(8,128)(2,1)} %bitcast.20, s32[768]{0:T(1024)S(1)} %fusion.54), kind=kOutput, calls=%fused_computation.17 | convolution fusion | flops 1813708800 | bytes 3542016 | tf_op jit(solution)/shard_map/dot_general | solution.py:15
  247.1 6.5 %collective-permute-done.7.refs_7_ = bf16[256,1536]{1,0:T(8,128)(2,1)S(1)} collective-permute-done((bf16[256,1536]{1,0:T(8,128)(2,1)S(1)}, bf16[256,1536]{1,0:T(8,128)(2,1)S(1)}, u32[]{:S(2)}, u32[]{:S(2)}) %collective-permute-start.7) | collective-permute-done | bytes 786464 | tf_op jit(solution)/shard_map/ppermute | solution.py:52
  254.5 11.3 %half_products.1 = (f32[768,1536]{1,0:T(8,128)}, f32[768,16]{1,0:T(8,128)}) custom-call(s32[2]{0:T(128)} %pad_add_fusion.where_ref, bf16[768,2048]{1,0:T(8,128)(2,1)} %bitcast.49, bf16[16,2048]{1,0:T(8,128)(2,1)} %get-tuple-element.43.first_ref, bf16[512,1536]{1,0:T(8,128)(2,1)} %copy-done.2, bf16[512,1536]{1,0:T(8,128)(2,1)} %copy-done.3, ...), custom_call_target="tpu_custom_call" | custom-call | tf_op jit(solution)/shard_map/half_products/pallas_call | solution.py:126
  266.8 17.2 %gradients.1 = f32[4,16,1408]{2,1,0:T(8,128)} custom-call(s32[2]{0:T(128)} %pad_add_fusion.where_ref, bf16[768,2048]{1,0:T(8,128)(2,1)} %bitcast.50, bf16[768,2048]{1,0:T(8,128)(2,1)} %bitcast.19.xb_ref, bf16[768,768]{1,0:T(8,128)(2,1)} %fusion.8.g0_ref, bf16[768,768]{1,0:T(8,128)(2,1)} %fusion.7.g1_ref, f32[768,1536]{1,0:T(8,128)} %get-tuple-element.33.frozen_ref, ...), custom_call_target="tpu_custom_call" | custom-call | tf_op jit(solution)/shard_map/gradients/pallas_call | solution.py:149
  284.0 10.9 %all_to_all.30 = f32[4,16,1408]{2,1,0:T(8,128)S(1)} all-to-all(f32[4,16,1408]{2,1,0:T(8,128)} %gradients.1), channel_id=1, replica_groups=mesh['zh'=4,'y'=4,'c'=2,'zl'=2,'x'=4] {'x'}, dimensions={0} | all-to-all | bytes 720896 | tf_op jit(solution)/shard_map/all_to_all | solution.py:268
  294.9 11.2 %all_to_all.31 = bf16[8,16,1408]{2,1,0:T(8,128)(2,1)S(1)} all-to-all(bf16[8,16,1408]{2,1,0:T(8,128)(2,1)S(1)} %broadcast_in_dim.5), channel_id=1, replica_groups=mesh['zh'=4,'y'=4,'c'=2,'zl'=2,'x'=4] {'zl','x'}, dimensions={0} | all-to-all | bytes 720896 | tf_op jit(solution)/shard_map/all_to_all | solution.py:271
  (72 shorter events, 21.7 us)
Async XLA Ops:
  7.2 170.9 %copy-start = (bf16[2,4096,16]{1,2,0:T(8,128)(2,1)S(1)}, bf16[2,4096,16]{1,2,0:T(8,128)(2,1)}, u32[]{:S(2)}) copy-start(bf16[2,4096,16]{1,2,0:T(8,128)(2,1)} %param.10) | copy-start | bytes 786436
  7.2 14.6 %copy-start.6 = (bf16[128,2,1536]{2,1,0:T(2,128)(2,1)S(1)}, bf16[128,2,1536]{2,1,0:T(2,128)(2,1)}, u32[]{:S(2)}) copy-start(bf16[128,2,1536]{2,1,0:T(2,128)(2,1)} %param.8) | copy-start | bytes 2359300
  7.2 108.1 %all-gather.3.cloned.1.call-start = ((), (), s32[]{:S(2)}) async-start(), calls=%async_computation.6 | async-start | bytes 4718592 | tf_op jit(solution)/shard_map/all_gather | solution.py:189
  11.8 18.8 %all-to-all-start = ((s32[8,2,128]{2,1,0:T(2,128)}), s32[8,2,128]{2,1,0:T(2,128)S(1)}, u32[]{:S(2)}, u32[]{:S(2)}) async-start(s32[8,2,128]{2,1,0:T(2,128)} %broadcast_in_dim.4), calls=%async_computation | async-start | bytes 16384 | tf_op jit(solution)/shard_map/all_to_all | solution.py:194
  20.3 169.7 %all-gather.5.cloned.1.call-start = ((), (), s32[]{:S(2)}) async-start(), calls=%async_computation.7 | async-start | bytes 4718592 | tf_op jit(solution)/shard_map/all_gather | solution.py:189
  26.3 17.0 %copy-start.2 = (bf16[512,1536]{1,0:T(8,128)(2,1)}, bf16[512,1536]{1,0:T(8,128)(2,1)S(1)}, u32[]{:S(2)}) copy-start(bf16[512,1536]{1,0:T(8,128)(2,1)S(1)} %get-tuple-element.37.refs_0_) | copy-start | bytes 4718596
  30.6 137.4 %all-to-all-start.1 = ((bf16[64,24,768]{2,1,0:T(8,128)(2,1)}), bf16[64,24,768]{2,1,0:T(8,128)(2,1)}, u32[]{:S(2)}, u32[]{:S(2)}) async-start(bf16[64,24,768]{2,1,0:T(8,128)(2,1)} %bitcast.53), calls=%async_computation.1 | async-start | bytes 4718592 | tf_op jit(solution)/shard_map/all_to_all | solution.py:214
  41.7 37.7 %collective-permute-start = (bf16[512,1536]{1,0:T(8,128)(2,1)S(1)}, bf16[512,1536]{1,0:T(8,128)(2,1)S(1)}, u32[]{:S(2)}, u32[]{:S(2)}) collective-permute-start(bf16[512,1536]{1,0:T(8,128)(2,1)S(1)} %get-tuple-element.37.refs_0_), channel_id=1, source_target_pairs={{0,1},{1,2},{2,3},{3,0},{4,5},{5,6},{6,7},{7,4},{8,9},{9,10},{10,1... | collective-permute-start | bytes 4718600 | tf_op jit(solution)/shard_map/ppermute | solution.py:47
  43.3 37.5 %collective-permute-start.2 = (bf16[512,1536]{1,0:T(8,128)(2,1)S(1)}, bf16[512,1536]{1,0:T(8,128)(2,1)S(1)}, u32[]{:S(2)}, u32[]{:S(2)}) collective-permute-start(bf16[512,1536]{1,0:T(8,128)(2,1)S(1)} %get-tuple-element.37.refs_0_), channel_id=1, source_target_pairs={{0,3},{1,0},{2,1},{3,2},{4,7},{5,4},{6,5},{7,6},{8,11},{9,8},{10,9... | collective-permute-start | bytes 4718600 | tf_op jit(solution)/shard_map/ppermute | solution.py:47
  45.0 123.0 %collective-permute-start.4 = (bf16[512,1536]{1,0:T(8,128)(2,1)}, bf16[512,1536]{1,0:T(8,128)(2,1)S(1)}, u32[]{:S(2)}, u32[]{:S(2)}) collective-permute-start(bf16[512,1536]{1,0:T(8,128)(2,1)} %get-tuple-element.24), channel_id=1, source_target_pairs={{0,4},{4,0},{1,5},{5,1},{2,6},{6,2},{3,7},{7,3},{8,12},{12,8},{9,1... | collective-permute-start | bytes 4718600 | tf_op jit(solution)/shard_map/ppermute | solution.py:200
  79.4 1.5 copy-start.3
  80.5 20.3 %collective-permute-start.1 = (bf16[256,1536]{1,0:T(8,128)(2,1)}, bf16[256,1536]{1,0:T(8,128)(2,1)}, u32[]{:S(2)}, u32[]{:S(2)}) collective-permute-start(bf16[256,1536]{1,0:T(8,128)(2,1)} %slice.116), channel_id=1, source_target_pairs={{0,1},{1,2},{2,3},{3,0},{4,5},{5,6},{6,7},{7,4},{8,9},{9,10},{10,1... | collective-permute-start | bytes 2359304 | tf_op jit(solution)/shard_map/ppermute | solution.py:52
  80.9 1.2 copy-start.4
  82.1 18.8 %collective-permute-start.3 = (bf16[256,1536]{1,0:T(8,128)(2,1)S(1)}, bf16[256,1536]{1,0:T(8,128)(2,1)S(1)}, u32[]{:S(2)}, u32[]{:S(2)}) collective-permute-start(bf16[256,1536]{1,0:T(8,128)(2,1)S(1)} %slice.117), channel_id=1, source_target_pairs={{0,3},{1,0},{2,1},{3,2},{4,7},{5,4},{6,5},{7,6},{8,11},{9,8},{10,9... | collective-permute-start | bytes 2359304 | tf_op jit(solution)/shard_map/ppermute | solution.py:52
  84.9 37.6 %copy-start.10 = (s32[768]{0:T(1024)}, s32[768]{0:T(1024)S(1)}, u32[]{:S(2)}) copy-start(s32[768]{0:T(1024)S(1)} %get-tuple-element.69) | copy-start | bytes 9220
  84.9 37.6 %copy-start.11 = (s32[1,8,128]{2,0,1:T(1,128)}, s32[1,8,128]{2,0,1:T(1,128)S(1)}, u32[]{:S(2)}) copy-start(s32[1,8,128]{2,0,1:T(1,128)S(1)} %get-tuple-element.60) | copy-start | bytes 12292
  84.9 37.6 %copy-start.12 = (s32[1,8,128]{2,0,1:T(1,128)}, s32[1,8,128]{2,0,1:T(1,128)S(1)}, u32[]{:S(2)}) copy-start(s32[1,8,128]{2,0,1:T(1,128)S(1)} %get-tuple-element.61) | copy-start | bytes 12292
  100.9 21.6 %copy-start.7 = (bf16[256,1536]{1,0:T(8,128)(2,1)}, bf16[256,1536]{1,0:T(8,128)(2,1)S(1)}, u32[]{:S(2)}) copy-start(bf16[256,1536]{1,0:T(8,128)(2,1)S(1)} %collective-permute-done.3.refs_3_) | copy-start | bytes 2359300
  168.0 1.2 copy-start.5
  169.2 50.2 %all-to-all-start.2 = ((bf16[8,96,2048]{2,1,0:T(8,128)(2,1)}), bf16[8,96,2048]{2,1,0:T(8,128)(2,1)S(1)}, u32[]{:S(2)}, u32[]{:S(2)}) async-start(bf16[8,96,2048]{2,1,0:T(8,128)(2,1)} %bitcast.52), calls=%async_computation.2 | async-start | bytes 6291456 | tf_op jit(solution)/shard_map/all_to_all | solution.py:229
  174.1 37.9 %collective-permute-start.5 = (bf16[512,1536]{1,0:T(8,128)(2,1)}, bf16[512,1536]{1,0:T(8,128)(2,1)}, u32[]{:S(2)}, u32[]{:S(2)}) collective-permute-start(bf16[512,1536]{1,0:T(8,128)(2,1)} %copy-done.5), channel_id=1, source_target_pairs={{0,1},{1,2},{2,3},{3,0},{4,5},{5,6},{6,7},{7,4},{8,9},{9,10},{10,1... | collective-permute-start | bytes 4718600 | tf_op jit(solution)/shard_map/ppermute | solution.py:47
  175.5 36.5 %collective-permute-start.6 = (bf16[512,1536]{1,0:T(8,128)(2,1)}, bf16[512,1536]{1,0:T(8,128)(2,1)}, u32[]{:S(2)}, u32[]{:S(2)}) collective-permute-start(bf16[512,1536]{1,0:T(8,128)(2,1)} %copy-done.5), channel_id=1, source_target_pairs={{0,3},{1,0},{2,1},{3,2},{4,7},{5,4},{6,5},{7,6},{8,11},{9,8},{10,9... | collective-permute-start | bytes 4718600 | tf_op jit(solution)/shard_map/ppermute | solution.py:47
  219.5 1.6 copy-start.1
  221.1 44.8 %all-to-all-start.3 = ((bf16[8,96,2048]{2,1,0:T(8,128)(2,1)}), bf16[8,96,2048]{2,1,0:T(8,128)(2,1)}, u32[]{:S(2)}, u32[]{:S(2)}) async-start(bf16[8,96,2048]{2,1,0:T(8,128)(2,1)} %bitcast.51), calls=%async_computation.3 | async-start | bytes 6291456 | tf_op jit(solution)/shard_map/all_to_all | solution.py:229
  232.7 20.9 %collective-permute-start.7 = (bf16[256,1536]{1,0:T(8,128)(2,1)S(1)}, bf16[256,1536]{1,0:T(8,128)(2,1)S(1)}, u32[]{:S(2)}, u32[]{:S(2)}) collective-permute-start(bf16[256,1536]{1,0:T(8,128)(2,1)S(1)} %slice.102), channel_id=1, source_target_pairs={{0,1},{1,2},{2,3},{3,0},{4,5},{5,6},{6,7},{7,4},{8,9},{9,10},{10,1... | collective-permute-start | bytes 2359304 | tf_op jit(solution)/shard_map/ppermute | solution.py:52
  235.4 30.4 %collective-permute-start.8 = (bf16[256,1536]{1,0:T(8,128)(2,1)S(1)}, bf16[256,1536]{1,0:T(8,128)(2,1)S(1)}, u32[]{:S(2)}, u32[]{:S(2)}) collective-permute-start(bf16[256,1536]{1,0:T(8,128)(2,1)S(1)} %slice.111), channel_id=1, source_target_pairs={{0,3},{1,0},{2,1},{3,2},{4,7},{5,4},{6,5},{7,6},{8,11},{9,8},{10,9... | collective-permute-start | bytes 2359304 | tf_op jit(solution)/shard_map/ppermute | solution.py:52
  253.6 0.9 copy-start.9
  265.8 0.9 copy-start.8
Sparse Core Ops, SparseCore 0:
  10.4 104.8 all-gather.2
  117.0 72.8 all-gather.4

commit v5 on v4

--- a/solution.py
+++ b/solution.py
@@ -5,10 +5,10 @@
 from jax.experimental.pallas import tpu as pltpu
 from jax.sharding import Mesh, PartitionSpec as P
 
+
 ADAPTER_SCALE = 2.0
 EXPERT_AXES = ("zh", "y", "c")
 DP_AXES = ("zl", "x")
-PLANE = ("zh", "y", "c", "zl")
 
 
 def dot(a, b, dims=((1,), (0,))):
@@ -27,16 +27,6 @@
     same = flat[:, None] == flat[None, :]
     ranks = jnp.sum((same & before).astype(jnp.int32), axis=1)
     return (flat * cap + ranks).reshape(top, rows)
-
-
-def send_places(experts, cap, swap):
-    p = jnp.arange(experts * 24, dtype=jnp.int32)
-    e, piece, r = p // 24, p % 24 // 8, p % 8
-    rank = jnp.where(piece < 2, r, 8 + r % 4)
-    half = jnp.where(piece < 2, piece, r // 4)
-    if swap:
-        half = jnp.where(e % 2 == 1, 1 - half, half)
-    return e * cap + rank, half
 
 
 RIGHT = [(i, (i + 1) % 4) for i in range(4)]
@@ -70,16 +60,16 @@
     low_ref[...] = dot(x_ref[...], first_ref[...], ((1,), (1,)))
 
 
-def final_kernel(where_ref, xa_ref, xb_ref, g0_ref, g1_ref, frozen_ref, lowa_ref, first_ref, second_ref, *refs):
+def final_kernel(where_ref, xa_ref, xb_ref, g_ref, frozen_ref, lowa_ref, first_ref, second_ref, *refs):
     out_ref, frozen_acc, slope_acc, sums = refs[8:]
     step = pl.program_id(0)
     low = (lowa_ref[...] + dot(xb_ref[...], first_ref[...], ((1,), (1,)))).astype(jnp.bfloat16)
     frozen_acc[...] = frozen_ref[...] + weight_products(where_ref, xb_ref, refs[:8])
-    half = g0_ref.shape[1]
-    for h, g_ref in enumerate((g0_ref, g1_ref)):
+    half = g_ref.shape[1] // 2
+    for h in range(2):
         cols = slice(h * half, (h + 1) * half)
         preact = frozen_acc[:, cols] + ADAPTER_SCALE * dot(low, second_ref[:, cols])
-        slope = g_ref[...].astype(jnp.float32) * silu_slope(preact)
+        slope = g_ref[:, cols].astype(jnp.float32) * silu_slope(preact)
         slope_acc[:, cols] = slope.astype(jnp.bfloat16)
     back = dot(slope_acc[...], second_ref[...], ((1,), (1,))).astype(jnp.bfloat16)
 
@@ -142,10 +132,10 @@
     )(where, x, first, *pieces)
 
 
-def gradients(where, xa, xb, g0, g1, frozen, low, first, second, pieces, h):
+def gradients(where, xa, xb, g, frozen, low, first, second, pieces, h):
     rows, hidden, rank = xa.shape[0], pieces[0].shape[1], first.shape[0]
     total = 2 * xa.shape[1] + hidden
-    by_row = [row_spec(v) for v in (xa, xb, g0, g1, frozen, low)]
+    by_row = [row_spec(v) for v in (xa, xb, g, frozen, low)]
     return pl.pallas_call(
         final_kernel,
         grid_spec=pltpu.PrefetchScalarGridSpec(
@@ -161,7 +151,7 @@
         ),
         out_shape=jax.ShapeDtypeStruct((4, rank, total // 4), jnp.float32),
         name="gradients",
-    )(where, xa, xb, g0, g1, frozen, low, first, second, *pieces)
+    )(where, xa, xb, g, frozen, low, first, second, *pieces)
 
 
 def split_kernel(tokens_ref, *out_refs):
@@ -179,7 +169,6 @@
 def local(tokens, route, gate_output_gradient, frozen_gate_weight, adapter_first, adapter_second):
     tok_rows, width = tokens.shape
     hidden = gate_output_gradient.shape[2]
-    experts = 64
     cap = 12
     depth = 8
     zh, zl, x = lax.axis_index("zh"), lax.axis_index("zl"), lax.axis_index("x")
@@ -199,23 +188,27 @@
     other, line_target = lax.optimization_barrier((other, line_target))
     got = lax.ppermute(other, "zl", [(0, 1), (1, 0)])
 
-    place, half = send_places(experts, cap, False)
-    match = place[:, None] == target.reshape(1, 2 * tok_rows)
-    pick_g = jnp.concatenate([match & (half == 0)[:, None], match & (half == 1)[:, None]], axis=1)
-    half_hidden = hidden // 2
-    parts = [
-        gate_output_gradient[:, k, h * half_hidden : (h + 1) * half_hidden]
-        for h in range(2)
-        for k in range(2)
-    ]
-    send_g = dot(pick_g.astype(jnp.bfloat16), jnp.concatenate(parts, axis=0)).astype(jnp.bfloat16)
-    send_g = send_g.reshape(experts, 24, half_hidden)
+    row = jnp.arange(depth * depth * cap, dtype=jnp.int32)
+    outer, inner, rank = row // (depth * cap), row // cap % depth, row % cap
+    zi = zh * 2 + zl
+    ahead = (zi + inner) % depth
+    key = ((ahead // 2 * depth + outer) * 2 + ahead % 2) * cap + rank
+    pick_g = key[:, None] == target.reshape(1, 2 * tok_rows)
+    slots = jnp.concatenate([gate_output_gradient[:, k] for k in range(2)], axis=0)
+    send_g = dot(pick_g.astype(jnp.bfloat16), slots).astype(jnp.bfloat16)
+    send_g = send_g.reshape(depth, depth * cap, hidden)
     send_g, line_target = lax.optimization_barrier((send_g, line_target))
-    recv_g = lax.all_to_all(send_g, PLANE, split_axis=0, concat_axis=0, tiled=True)
+    column_g = lax.all_to_all(send_g, ("y", "c"), split_axis=0, concat_axis=0, tiled=True)
+    swapped = (inner * depth + outer) * cap + rank
+    swap = (swapped[:, None] == row[None, :]).astype(jnp.bfloat16)
+    column_g = dot(swap, column_g.reshape(-1, hidden)).astype(jnp.bfloat16)
+    blocks_g = [column_g[n * depth * cap : (n + 1) * depth * cap] for n in range(depth)]
+    for n in (4, 3, 5, 2, 6, 1, 7):
+        moves = [(i, (i + n) % depth) for i in range(depth)]
+        blocks_g[n] = lax.ppermute(blocks_g[n], ("zh", "zl"), moves)
 
     line_target = line_target.transpose(1, 0, 2).reshape(2, depth * tok_rows)
-    row = jnp.arange(depth * depth * cap, dtype=jnp.int32)
-    served = (zh * depth + row // (depth * cap)) * 2 + zl
+    served = (zh * depth + outer) * 2 + zl
     key = (served * cap + row % cap)[:, None]
     col = jnp.arange(depth * tok_rows, dtype=jnp.int32)
     same_block = (row // cap % depth)[:, None] == (col // tok_rows)[None, :]
@@ -230,22 +223,18 @@
         return rows.reshape(depth * depth * cap, half_width)
 
     near_opposite = second_hop(*near)
-    line0, near_opposite = lax.optimization_barrier((lines[0], near_opposite))
-    send_0, recv_g, got = lax.optimization_barrier((packed(line0), recv_g, got))
+    line0, near_opposite, column_g = lax.optimization_barrier((lines[0], near_opposite, column_g))
     far = first_hop(got)
+    send_0, far = lax.optimization_barrier((packed(line0), far))
+    far_opposite = second_hop(*far)
     xa = spread(send_0)
-    line1, far = lax.optimization_barrier((lines[1], far))
-    far_opposite = second_hop(*far)
+    line1, far_opposite = lax.optimization_barrier((lines[1], far_opposite))
     xb = spread(packed(line1))
 
-    recv_g = recv_g.reshape(experts * 24, half_hidden)
-    block, rank = row // cap, row % cap
-    source = block // 2 % 4 * 16 + block // 8 * 2 + block % 2
-    q = jnp.arange(experts * 24, dtype=jnp.int32)
-
-    def gather_half(h):
-        at = source * 24 + jnp.where(rank < 8, 8 * h + rank, 16 + 4 * h + rank - 8)
-        return dot((at[:, None] == q[None, :]).astype(jnp.bfloat16), recv_g).astype(jnp.bfloat16)
+    behind = (zi - inner) % depth
+    order = (behind * depth + outer) * cap + rank
+    order = (order[:, None] == row[None, :]).astype(jnp.bfloat16)
+    rows_g = dot(order, jnp.concatenate(blocks_g, axis=0)).astype(jnp.bfloat16)
 
     first = lax.dynamic_index_in_dim(adapter_first, zl, 0, keepdims=False)
     second = lax.dynamic_index_in_dim(adapter_second, zl, 0, keepdims=False)
@@ -260,9 +249,7 @@
         for h in range(2)
     ]
     frozen, low = half_products(where, xa, first_a, pieces[0], 0)
-    parts = gradients(
-        where, xa, xb, gather_half(0), gather_half(1), frozen, low, first_b, second, pieces[1], 1
-    )
+    parts = gradients(where, xa, xb, rows_g, frozen, low, first_b, second, pieces[1], 1)
 
     rank, chunk = parts.shape[1:]
     parts = lax.all_to_all(parts, "x", split_axis=0, concat_axis=0, tiled=True)

time: 315 us -> 339 us (1.076)
  waiting for transfers between devices: 149 us -> 168 us
  starting transfers between devices: 43.7 us -> 54.5 us
  local copies, waits for them, and re-layouts: 20.8 us -> 15.9 us
    ppermute x4, waiting for transfers between devices: 55 us -> 0.01 us  [first_hop(): return (lax.ppermute(shard, 'x', RIGHT), lax.ppermute(shard, 'x', LEFT))]
    ppermute x0 -> x7, waiting for transfers between devices: none -> 44.5 us  [local(): blocks_g[n] = lax.ppermute(blocks_g[n], ('zh', 'zl'), moves)]
    ppermute x2, waiting for transfers between devices: 22.3 us -> 55.7 us  [second_hop(): lax.ppermute(before[:half], 'x', RIGHT)]
    all_gather x2, waiting for transfers between devices: 25.6 us -> 0.01 us  [local(): lax.all_gather(part, ('zh', 'zl'), axis=0, tiled=True)]
    ppermute x0 -> x7, starting transfers between devices: none -> 15.4 us  [local(): blocks_g[n] = lax.ppermute(blocks_g[n], ('zh', 'zl'), moves)]
    ppermute x1, waiting for transfers between devices: 45.5 us -> 60.8 us  [local(): got = lax.ppermute(other, 'zl', [(0, 1), (1, 0)])]
    unnamed x33 -> x37, local copies, waits for them, and re-layouts: 10.1 us -> 1.84 us
    all_to_all x1, starting transfers between devices: 11.1 us -> 4.92 us  [local(): lax.all_to_all(send_g, ('y', 'c'), split_axis=0, concat_axis=0, tiled=True)]
  transfers between devices with their start and end apart: 15 -> 22, of which waited for: 8 -> 10; matrix products, arithmetic and copies ran while one was open for 15% -> 13% of each run, Pallas kernels for 4% -> 3%
where the time goes in v5:
time: 339 us
  waiting for transfers between devices  168 us (50%)
  starting transfers between devices  54.5 us (16%)
  Pallas kernels  31.3 us (9%)
  matrix products  25.6 us (8%)
  blocking collectives  24.2 us (7%)
  local copies, waits for them, and re-layouts  15.9 us (5%)
  between operations  14.3 us (4%)
  other arithmetic  4.6 us (1%)
    ppermute x1, waiting for transfers between devices, local(): got = lax.ppermute(other, 'zl', [(0, 1), (1, 0)])  60.8 us
    ppermute x2, waiting for transfers between devices, second_hop(): lax.ppermute(before[:half], 'x', RIGHT)  55.7 us
    ppermute x7, waiting for transfers between devices, local(): blocks_g[n] = lax.ppermute(blocks_g[n], ('zh', 'zl'), moves)  44.5 us
    dot_general x5, matrix products, dot(): lax.dot_general(a, b, (dims, ((), ())), preferred_element_type=jnp.float32)  25.6 us
    pallas_call x1, Pallas kernels, gradients(): pl.pallas_call(final_kernel, grid_spec=pltpu.PrefetchScalarGridSpec(num_s...  17.7 us
    ppermute x7, starting transfers between devices, local(): blocks_g[n] = lax.ppermute(blocks_g[n], ('zh', 'zl'), moves)  15.4 us
    all_to_all x1, blocking collectives, local(): lax.all_to_all(total, DP_AXES, split_axis=0, concat_axis=0, tiled=True)  12.9 us
    all_to_all x1, blocking collectives, local(): parts = lax.all_to_all(parts, 'x', split_axis=0, concat_axis=0, tiled=True)  11.3 us
  transfers between devices with their start and end apart: 22, of which 10 were waited for; matrix products, arithmetic and copies ran while one was open for 13% of the time, Pallas kernels for 3%

profile of v5, /device:TPU:8, one launch (start us, length us, event | category | flops | bytes accessed | tf_op | source)
XLA Modules:
  0.0 338.6 jit_solution(5028574501525279804)
XLA Ops:
  7.2 2.3 split_columns.1
  11.8 8.5 %all-to-all-start = ((s32[8,2,128]{2,1,0:T(2,128)}), s32[8,2,128]{2,1,0:T(2,128)S(1)}, u32[]{:S(2)}, u32[]{:S(2)}) async-start(s32[8,2,128]{2,1,0:T(2,128)} %broadcast_in_dim.4), calls=%async_computation | async-start | bytes 16384 | tf_op jit(solution)/shard_map/all_to_all | solution.py:183
  21.7 3.3 dynamic-slice_bitcast_fusion.1
  26.3 2.2 convolution_convert_fusion.2
  28.5 4.9 %all-to-all-start.1 = ((bf16[8,96,1536]{2,1,0:T(8,128)(2,1)}), bf16[8,96,1536]{2,1,0:T(8,128)(2,1)}, u32[]{:S(2)}, u32[]{:S(2)}) async-start(bf16[8,96,1536]{2,1,0:T(8,128)(2,1)} %bitcast.47), calls=%async_computation.1 | async-start | bytes 4718592 | tf_op jit(solution)/shard_map/all_to_all | solution.py:201
  38.7 60.8 %collective-permute-done.4.refs_4_ = bf16[512,1536]{1,0:T(8,128)(2,1)} collective-permute-done((bf16[512,1536]{1,0:T(8,128)(2,1)}, bf16[512,1536]{1,0:T(8,128)(2,1)}, u32[]{:S(2)}, u32[]{:S(2)}) %collective-permute-start.4) | collective-permute-done | bytes 1572896 | tf_op jit(solution)/shard_map/ppermute | solution.py:189
  105.3 3.1 collective-permute-start.3
  108.4 5.2 %convolution_convert_fusion.4 = bf16[768,1536]{1,0:T(8,128)(2,1)} fusion(bf16[768,1536]{1,0:T(8,128)(2,1)} %bitcast.14, s32[768]{0:T(1024)S(1)} %fusion.29), kind=kOutput, calls=%fused_computation.4 | convolution fusion | flops 1813708800 | bytes 4721664 | tf_op jit(solution)/shard_map/dot_general | solution.py:15
  113.5 40.6 %collective-permute-done.1.refs_3_ = bf16[256,1536]{1,0:T(8,128)(2,1)} collective-permute-done((bf16[256,1536]{1,0:T(8,128)(2,1)}, bf16[256,1536]{1,0:T(8,128)(2,1)}, u32[]{:S(2)}, u32[]{:S(2)}) %collective-permute-start.1) | collective-permute-done | bytes 786464 | tf_op jit(solution)/shard_map/ppermute | solution.py:42
  154.1 7.5 %convolution_convert_fusion.1 = bf16[768,2048]{1,0:T(8,128)(2,1)} fusion(bf16[1024,2048]{1,0:T(8,128)(2,1)} %all-gather.3.cloned.1.call-done, s32[1024]{0:T(1024)S(1)} %bitcast.57, s32[1024]{0:T(1024)S(1)} %bitcast.55, s32[1024]{0:T(1024)S(1)} %add_select_fusion.5, s32[768]{0:T(1024)S(1)} %get-tuple-element.68, s32[768]{0:T(1024)S(1)} %get-tuple-element.69), kind=kOutput, calls=%fused_computation.1 | convolution fusion | flops 3226730496 | bytes 7358464 | tf_op jit(solution)/shard_map/dot_general | solution.py:15
  161.7 4.8 %all-to-all-start.2 = ((bf16[8,96,2048]{2,1,0:T(8,128)(2,1)}), bf16[8,96,2048]{2,1,0:T(8,128)(2,1)S(1)}, u32[]{:S(2)}, u32[]{:S(2)}) async-start(bf16[8,96,2048]{2,1,0:T(8,128)(2,1)} %bitcast.49), calls=%async_computation.2 | async-start | bytes 6291456 | tf_op jit(solution)/shard_map/all_to_all | solution.py:222
  166.6 2.1 slice.110
  170.0 2.1 slice.111
  174.7 15.1 %collective-permute-done.7.refs_7_ = bf16[256,1536]{1,0:T(8,128)(2,1)} collective-permute-done((bf16[256,1536]{1,0:T(8,128)(2,1)}, bf16[256,1536]{1,0:T(8,128)(2,1)}, u32[]{:S(2)}, u32[]{:S(2)}) %collective-permute-start.7) | collective-permute-done | bytes 786464 | tf_op jit(solution)/shard_map/ppermute | solution.py:42
  191.7 7.2 %convolution_convert_fusion = bf16[768,2048]{1,0:T(8,128)(2,1)} fusion(bf16[1024,2048]{1,0:T(8,128)(2,1)} %all-gather.5.cloned.1.call-done, s32[1024]{0:T(1024)S(1)} %bitcast.58, s32[1024]{0:T(1024)S(1)} %bitcast.56, s32[1024]{0:T(1024)S(1)} %add_select_fusion.5, s32[768]{0:T(1024)S(1)} %get-tuple-element.68, s32[768]{0:T(1024)S(1)} %get-tuple-element.69), kind=kOutput, calls=%fused_computation | convolution fusion | flops 3226730496 | bytes 7358464 | tf_op jit(solution)/shard_map/dot_general | solution.py:15
  198.8 4.6 %all-to-all-done.2 = bf16[8,96,2048]{2,1,0:T(8,128)(2,1)S(1)} async-done(((bf16[8,96,2048]{2,1,0:T(8,128)(2,1)}), bf16[8,96,2048]{2,1,0:T(8,128)(2,1)S(1)}, u32[]{:S(2)}, u32[]{:S(2)}) %all-to-all-start.2) | async-done | bytes 3145760 | tf_op jit(solution)/shard_map/all_to_all | solution.py:222
  205.1 5.8 %all-to-all-start.3 = ((bf16[8,96,2048]{2,1,0:T(8,128)(2,1)}), bf16[8,96,2048]{2,1,0:T(8,128)(2,1)}, u32[]{:S(2)}, u32[]{:S(2)}) async-start(bf16[8,96,2048]{2,1,0:T(8,128)(2,1)} %bitcast.48), calls=%async_computation.3 | async-start | bytes 6291456 | tf_op jit(solution)/shard_map/all_to_all | solution.py:222
  213.6 2.1 collective-permute-start.10
  216.4 3.3 collective-permute-start.11
  219.7 2.7 collective-permute-start.12
  222.4 3.0 collective-permute-start.13
  225.4 3.4 %collective-permute-start.14 = (bf16[96,1536]{1,0:T(8,128)(2,1)S(1)}, bf16[96,1536]{1,0:T(8,128)(2,1)S(1)}, u32[]{:S(2)}, u32[]{:S(2)}) collective-permute-start(bf16[96,1536]{1,0:T(8,128)(2,1)S(1)} %get-tuple-element.39), channel_id=1, source_target_pairs={{0,192},{4,196},{64,0},{68,4},{128,64},{132,68},{192,128},{196,132... | collective-permute-start | bytes 884744 | tf_op jit(solution)/shard_map/ppermute | solution.py:208
  228.8 14.7 %collective-permute-done.10 = bf16[96,1536]{1,0:T(8,128)(2,1)S(1)} collective-permute-done((bf16[96,1536]{1,0:T(8,128)(2,1)S(1)}, bf16[96,1536]{1,0:T(8,128)(2,1)S(1)}, u32[]{:S(2)}, u32[]{:S(2)}) %collective-permute-start.10) | collective-permute-done | bytes 294944 | tf_op jit(solution)/shard_map/ppermute | solution.py:208
  243.5 11.3 %collective-permute-done.11 = bf16[96,1536]{1,0:T(8,128)(2,1)S(1)} collective-permute-done((bf16[96,1536]{1,0:T(8,128)(2,1)S(1)}, bf16[96,1536]{1,0:T(8,128)(2,1)S(1)}, u32[]{:S(2)}, u32[]{:S(2)}) %collective-permute-start.11) | collective-permute-done | bytes 294944 | tf_op jit(solution)/shard_map/ppermute | solution.py:208
  254.9 9.9 %collective-permute-done.12 = bf16[96,1536]{1,0:T(8,128)(2,1)S(1)} collective-permute-done((bf16[96,1536]{1,0:T(8,128)(2,1)S(1)}, bf16[96,1536]{1,0:T(8,128)(2,1)S(1)}, u32[]{:S(2)}, u32[]{:S(2)}) %collective-permute-start.12) | collective-permute-done | bytes 294944 | tf_op jit(solution)/shard_map/ppermute | solution.py:208
  264.8 4.7 %collective-permute-done.14 = bf16[96,1536]{1,0:T(8,128)(2,1)S(1)} collective-permute-done((bf16[96,1536]{1,0:T(8,128)(2,1)S(1)}, bf16[96,1536]{1,0:T(8,128)(2,1)S(1)}, u32[]{:S(2)}, u32[]{:S(2)}) %collective-permute-start.14) | collective-permute-done | bytes 294944 | tf_op jit(solution)/shard_map/ppermute | solution.py:208
  269.5 3.9 %collective-permute-done.15 = bf16[96,1536]{1,0:T(8,128)(2,1)S(1)} collective-permute-done((bf16[96,1536]{1,0:T(8,128)(2,1)S(1)}, bf16[96,1536]{1,0:T(8,128)(2,1)S(1)}, u32[]{:S(2)}, u32[]{:S(2)}) %collective-permute-start.15) | collective-permute-done | bytes 294944 | tf_op jit(solution)/shard_map/ppermute | solution.py:208
  273.4 3.5 %convolution_convert_fusion.3.g_ref = bf16[768,1536]{1,0:T(8,128)(2,1)} fusion(bf16[768,1536]{1,0:T(8,128)(2,1)S(1)} %constant_dynamic-update-slice_fusion, s32[768]{0:T(1024)S(1)} %fusion.28), kind=kOutput, calls=%fused_computation.3 | convolution fusion | flops 1813708800 | bytes 4721664 | tf_op jit(solution)/shard_map/dot_general | solution.py:15
  276.9 11.3 %half_products.1 = (f32[768,1536]{1,0:T(8,128)}, f32[768,16]{1,0:T(8,128)}) custom-call(s32[2]{0:T(128)} %pad_add_fusion.where_ref, bf16[768,2048]{1,0:T(8,128)(2,1)} %bitcast.45, bf16[16,2048]{1,0:T(8,128)(2,1)} %copy-done.8, bf16[512,1536]{1,0:T(8,128)(2,1)} %copy-done.3, bf16[512,1536]{1,0:T(8,128)(2,1)} %copy-done.4, ...), custom_call_target="tpu_custom_call" | custom-call | tf_op jit(solution)/shard_map/half_products/pallas_call | solution.py:116
  288.2 17.7 %gradients.1 = f32[4,16,1408]{2,1,0:T(8,128)} custom-call(s32[2]{0:T(128)} %pad_add_fusion.where_ref, bf16[768,2048]{1,0:T(8,128)(2,1)} %bitcast.46, bf16[768,2048]{1,0:T(8,128)(2,1)} %bitcast.18.xb_ref, bf16[768,1536]{1,0:T(8,128)(2,1)} %convolution_convert_fusion.3.g_ref, f32[768,1536]{1,0:T(8,128)} %get-tuple-element.32.frozen_ref, ...), custom_call_target="tpu_custom_call" | custom-call | tf_op jit(solution)/shard_map/gradients/pallas_call | solution.py:139
  306.0 11.3 %all_to_all.30 = f32[4,16,1408]{2,1,0:T(8,128)S(1)} all-to-all(f32[4,16,1408]{2,1,0:T(8,128)} %gradients.1), channel_id=1, replica_groups=mesh['zh'=4,'y'=4,'c'=2,'zl'=2,'x'=4] {'x'}, dimensions={0} | all-to-all | bytes 720896 | tf_op jit(solution)/shard_map/all_to_all | solution.py:255
  317.4 12.9 %all_to_all.31 = bf16[8,16,1408]{2,1,0:T(8,128)(2,1)S(1)} all-to-all(bf16[8,16,1408]{2,1,0:T(8,128)(2,1)S(1)} %broadcast_in_dim.5), channel_id=1, replica_groups=mesh['zh'=4,'y'=4,'c'=2,'zl'=2,'x'=4] {'zl','x'}, dimensions={0} | all-to-all | bytes 720896 | tf_op jit(solution)/shard_map/all_to_all | solution.py:258
  (89 shorter events, 28.6 us)
Async XLA Ops:
  7.2 159.3 %copy-start = (bf16[2,4096,16]{1,2,0:T(8,128)(2,1)S(1)}, bf16[2,4096,16]{1,2,0:T(8,128)(2,1)}, u32[]{:S(2)}) copy-start(bf16[2,4096,16]{1,2,0:T(8,128)(2,1)} %param.10) | copy-start | bytes 786436
  7.2 146.9 %all-gather.3.cloned.1.call-start = ((), (), s32[]{:S(2)}) async-start(), calls=%async_computation.6 | async-start | bytes 4718592 | tf_op jit(solution)/shard_map/all_gather | solution.py:178
  11.8 16.7 %all-to-all-start = ((s32[8,2,128]{2,1,0:T(2,128)}), s32[8,2,128]{2,1,0:T(2,128)S(1)}, u32[]{:S(2)}, u32[]{:S(2)}) async-start(s32[8,2,128]{2,1,0:T(2,128)} %broadcast_in_dim.4), calls=%async_computation | async-start | bytes 16384 | tf_op jit(solution)/shard_map/all_to_all | solution.py:183
  20.2 154.4 %all-gather.5.cloned.1.call-start = ((), (), s32[]{:S(2)}) async-start(), calls=%async_computation.7 | async-start | bytes 4718592 | tf_op jit(solution)/shard_map/all_gather | solution.py:178
  25.1 11.9 %copy-start.3 = (bf16[512,1536]{1,0:T(8,128)(2,1)}, bf16[512,1536]{1,0:T(8,128)(2,1)S(1)}, u32[]{:S(2)}) copy-start(bf16[512,1536]{1,0:T(8,128)(2,1)S(1)} %get-tuple-element.37.refs_0_) | copy-start | bytes 4718596
  28.5 79.9 %all-to-all-start.1 = ((bf16[8,96,1536]{2,1,0:T(8,128)(2,1)}), bf16[8,96,1536]{2,1,0:T(8,128)(2,1)}, u32[]{:S(2)}, u32[]{:S(2)}) async-start(bf16[8,96,1536]{2,1,0:T(8,128)(2,1)} %bitcast.47), calls=%async_computation.1 | async-start | bytes 4718592 | tf_op jit(solution)/shard_map/all_to_all | solution.py:201
  33.4 66.1 %collective-permute-start.4 = (bf16[512,1536]{1,0:T(8,128)(2,1)}, bf16[512,1536]{1,0:T(8,128)(2,1)}, u32[]{:S(2)}, u32[]{:S(2)}) collective-permute-start(bf16[512,1536]{1,0:T(8,128)(2,1)} %get-tuple-element.24), channel_id=1, source_target_pairs={{0,4},{4,0},{1,5},{5,1},{2,6},{6,2},{3,7},{7,3},{8,12},{12,8},{9,1... | collective-permute-start | bytes 4718600 | tf_op jit(solution)/shard_map/ppermute | solution.py:189
  35.4 67.3 %collective-permute-start = (bf16[512,1536]{1,0:T(8,128)(2,1)S(1)}, bf16[512,1536]{1,0:T(8,128)(2,1)S(1)}, u32[]{:S(2)}, u32[]{:S(2)}) collective-permute-start(bf16[512,1536]{1,0:T(8,128)(2,1)S(1)} %get-tuple-element.37.refs_0_), channel_id=1, source_target_pairs={{0,1},{1,2},{2,3},{3,0},{4,5},{5,6},{6,7},{7,4},{8,9},{9,10},{10,1... | collective-permute-start | bytes 4718600 | tf_op jit(solution)/shard_map/ppermute | solution.py:37
  36.9 67.2 %collective-permute-start.2 = (bf16[512,1536]{1,0:T(8,128)(2,1)S(1)}, bf16[512,1536]{1,0:T(8,128)(2,1)}, u32[]{:S(2)}, u32[]{:S(2)}) collective-permute-start(bf16[512,1536]{1,0:T(8,128)(2,1)S(1)} %get-tuple-element.37.refs_0_), channel_id=1, source_target_pairs={{0,3},{1,0},{2,1},{3,2},{4,7},{5,4},{6,5},{7,6},{8,11},{9,8},{10,9... | collective-permute-start | bytes 4718600 | tf_op jit(solution)/shard_map/ppermute | solution.py:37
  99.5 62.2 %collective-permute-start.5 = (bf16[512,1536]{1,0:T(8,128)(2,1)}, bf16[512,1536]{1,0:T(8,128)(2,1)}, u32[]{:S(2)}, u32[]{:S(2)}) collective-permute-start(bf16[512,1536]{1,0:T(8,128)(2,1)} %collective-permute-done.4.refs_4_), channel_id=1, source_target_pairs={{0,1},{1,2},{2,3},{3,0},{4,5},{5,6},{6,7},{7,4},{8,9},{9,10},{10,1... | collective-permute-start | bytes 4718600 | tf_op jit(solution)/shard_map/ppermute | solution.py:37
  101.0 60.7 %collective-permute-start.6 = (bf16[512,1536]{1,0:T(8,128)(2,1)}, bf16[512,1536]{1,0:T(8,128)(2,1)}, u32[]{:S(2)}, u32[]{:S(2)}) collective-permute-start(bf16[512,1536]{1,0:T(8,128)(2,1)} %collective-permute-done.4.refs_4_), channel_id=1, source_target_pairs={{0,3},{1,0},{2,1},{3,2},{4,7},{5,4},{6,5},{7,6},{8,11},{9,8},{10,9... | collective-permute-start | bytes 4718600 | tf_op jit(solution)/shard_map/ppermute | solution.py:37
  102.7 10.8 %copy-start.4 = (bf16[512,1536]{1,0:T(8,128)(2,1)}, bf16[512,1536]{1,0:T(8,128)(2,1)S(1)}, u32[]{:S(2)}) copy-start(bf16[512,1536]{1,0:T(8,128)(2,1)S(1)} %collective-permute-done.refs_1_) | copy-start | bytes 4718596
  103.8 50.3 %collective-permute-start.1 = (bf16[256,1536]{1,0:T(8,128)(2,1)}, bf16[256,1536]{1,0:T(8,128)(2,1)}, u32[]{:S(2)}, u32[]{:S(2)}) collective-permute-start(bf16[256,1536]{1,0:T(8,128)(2,1)} %slice.140), channel_id=1, source_target_pairs={{0,1},{1,2},{2,3},{3,0},{4,5},{5,6},{6,7},{7,4},{8,9},{9,10},{10,1... | collective-permute-start | bytes 2359304 | tf_op jit(solution)/shard_map/ppermute | solution.py:42
  105.3 48.8 %collective-permute-start.3 = (bf16[256,1536]{1,0:T(8,128)(2,1)S(1)}, bf16[256,1536]{1,0:T(8,128)(2,1)S(1)}, u32[]{:S(2)}, u32[]{:S(2)}) collective-permute-start(bf16[256,1536]{1,0:T(8,128)(2,1)S(1)} %slice.141), channel_id=1, source_target_pairs={{0,3},{1,0},{2,1},{3,2},{4,7},{5,4},{6,5},{7,6},{8,11},{9,8},{10,9... | collective-permute-start | bytes 2359304 | tf_op jit(solution)/shard_map/ppermute | solution.py:42
  108.3 45.8 %copy-start.10 = (s32[1,8,128]{2,0,1:T(1,128)}, s32[1,8,128]{2,0,1:T(1,128)S(1)}, u32[]{:S(2)}) copy-start(s32[1,8,128]{2,0,1:T(1,128)S(1)} %get-tuple-element.65) | copy-start | bytes 12292
  154.1 7.5 %copy-start.6 = (bf16[256,1536]{1,0:T(8,128)(2,1)}, bf16[256,1536]{1,0:T(8,128)(2,1)S(1)}, u32[]{:S(2)}) copy-start(bf16[256,1536]{1,0:T(8,128)(2,1)S(1)} %collective-permute-done.3.refs_3_) | copy-start | bytes 2359300
  161.7 41.8 %all-to-all-start.2 = ((bf16[8,96,2048]{2,1,0:T(8,128)(2,1)}), bf16[8,96,2048]{2,1,0:T(8,128)(2,1)S(1)}, u32[]{:S(2)}, u32[]{:S(2)}) async-start(bf16[8,96,2048]{2,1,0:T(8,128)(2,1)} %bitcast.49), calls=%async_computation.2 | async-start | bytes 6291456 | tf_op jit(solution)/shard_map/all_to_all | solution.py:222
  166.5 7.5 %copy-start.9 = (bf16[2,16,1536]{2,1,0:T(8,128)(2,1)S(1)}, bf16[2,16,1536]{2,1,0:T(8,128)(2,1)}, u32[]{:S(2)}) copy-start(bf16[2,16,1536]{2,1,0:T(8,128)(2,1)} %param.11) | copy-start | bytes 294916
  166.5 25.1 %copy-start.11 = (s32[1,8,128]{2,0,1:T(1,128)S(1)}, s32[1,8,128]{2,0,1:T(1,128)}, u32[]{:S(2)}) copy-start(s32[1,8,128]{2,0,1:T(1,128)} %copy-done.10) | copy-start | bytes 12292
  168.7 21.1 %collective-permute-start.7 = (bf16[256,1536]{1,0:T(8,128)(2,1)}, bf16[256,1536]{1,0:T(8,128)(2,1)}, u32[]{:S(2)}, u32[]{:S(2)}) collective-permute-start(bf16[256,1536]{1,0:T(8,128)(2,1)} %slice.110), channel_id=1, source_target_pairs={{0,1},{1,2},{2,3},{3,0},{4,5},{5,6},{6,7},{7,4},{8,9},{9,10},{10,1... | collective-permute-start | bytes 2359304 | tf_op jit(solution)/shard_map/ppermute | solution.py:42
  172.1 19.6 %collective-permute-start.8 = (bf16[256,1536]{1,0:T(8,128)(2,1)}, bf16[256,1536]{1,0:T(8,128)(2,1)}, u32[]{:S(2)}, u32[]{:S(2)}) collective-permute-start(bf16[256,1536]{1,0:T(8,128)(2,1)} %slice.111), channel_id=1, source_target_pairs={{0,3},{1,0},{2,1},{3,2},{4,7},{5,4},{6,5},{7,6},{8,11},{9,8},{10,9... | collective-permute-start | bytes 2359304 | tf_op jit(solution)/shard_map/ppermute | solution.py:42
  205.1 83.1 %all-to-all-start.3 = ((bf16[8,96,2048]{2,1,0:T(8,128)(2,1)}), bf16[8,96,2048]{2,1,0:T(8,128)(2,1)}, u32[]{:S(2)}, u32[]{:S(2)}) async-start(bf16[8,96,2048]{2,1,0:T(8,128)(2,1)} %bitcast.48), calls=%async_computation.3 | async-start | bytes 6291456 | tf_op jit(solution)/shard_map/all_to_all | solution.py:222
  212.7 12.6 %collective-permute-start.9 = (bf16[96,1536]{1,0:T(8,128)(2,1)S(1)}, bf16[96,1536]{1,0:T(8,128)(2,1)S(1)}, u32[]{:S(2)}, u32[]{:S(2)}) collective-permute-start(bf16[96,1536]{1,0:T(8,128)(2,1)S(1)} %get-tuple-element.44), channel_id=1, source_target_pairs={{0,4},{4,64},{64,68},{68,128},{128,132},{132,192},{192,196},{196,0... | collective-permute-start | bytes 884744 | tf_op jit(solution)/shard_map/ppermute | solution.py:208
  213.6 63.3 %copy-start.7 = (bf16[16,2048]{1,0:T(8,128)(2,1)}, bf16[16,2048]{1,0:T(8,128)(2,1)S(1)}, u32[]{:S(2)}) copy-start(bf16[16,2048]{1,0:T(8,128)(2,1)S(1)} %get-tuple-element.48.first_ref) | copy-start | bytes 196612
  213.6 63.3 %copy-start.8 = (bf16[16,2048]{1,0:T(8,128)(2,1)}, bf16[16,2048]{1,0:T(8,128)(2,1)S(1)}, u32[]{:S(2)}) copy-start(bf16[16,2048]{1,0:T(8,128)(2,1)S(1)} %get-tuple-element.49.first_ref) | copy-start | bytes 196612
  213.6 29.8 %collective-permute-start.10 = (bf16[96,1536]{1,0:T(8,128)(2,1)S(1)}, bf16[96,1536]{1,0:T(8,128)(2,1)S(1)}, u32[]{:S(2)}, u32[]{:S(2)}) collective-permute-start(bf16[96,1536]{1,0:T(8,128)(2,1)S(1)} %get-tuple-element.43), channel_id=1, source_target_pairs={{0,64},{4,68},{64,128},{68,132},{128,192},{132,196},{192,0},{196,4... | collective-permute-start | bytes 884744 | tf_op jit(solution)/shard_map/ppermute | solution.py:208
  216.4 38.5 %collective-permute-start.11 = (bf16[96,1536]{1,0:T(8,128)(2,1)S(1)}, bf16[96,1536]{1,0:T(8,128)(2,1)S(1)}, u32[]{:S(2)}, u32[]{:S(2)}) collective-permute-start(bf16[96,1536]{1,0:T(8,128)(2,1)S(1)} %get-tuple-element.42), channel_id=1, source_target_pairs={{0,68},{4,128},{64,132},{68,192},{128,196},{132,0},{192,4},{196,64... | collective-permute-start | bytes 884744 | tf_op jit(solution)/shard_map/ppermute | solution.py:208
  219.7 45.1 %collective-permute-start.12 = (bf16[96,1536]{1,0:T(8,128)(2,1)S(1)}, bf16[96,1536]{1,0:T(8,128)(2,1)S(1)}, u32[]{:S(2)}, u32[]{:S(2)}) collective-permute-start(bf16[96,1536]{1,0:T(8,128)(2,1)S(1)} %get-tuple-element.41), channel_id=1, source_target_pairs={{0,128},{4,132},{64,192},{68,196},{128,0},{132,4},{192,64},{196,68... | collective-permute-start | bytes 884744 | tf_op jit(solution)/shard_map/ppermute | solution.py:208
  222.4 42.4 %collective-permute-start.13 = (bf16[96,1536]{1,0:T(8,128)(2,1)S(1)}, bf16[96,1536]{1,0:T(8,128)(2,1)S(1)}, u32[]{:S(2)}, u32[]{:S(2)}) collective-permute-start(bf16[96,1536]{1,0:T(8,128)(2,1)S(1)} %get-tuple-element.40), channel_id=1, source_target_pairs={{0,132},{4,192},{64,196},{68,0},{128,4},{132,64},{192,68},{196,128... | collective-permute-start | bytes 884744 | tf_op jit(solution)/shard_map/ppermute | solution.py:208
  225.4 44.1 %collective-permute-start.14 = (bf16[96,1536]{1,0:T(8,128)(2,1)S(1)}, bf16[96,1536]{1,0:T(8,128)(2,1)S(1)}, u32[]{:S(2)}, u32[]{:S(2)}) collective-permute-start(bf16[96,1536]{1,0:T(8,128)(2,1)S(1)} %get-tuple-element.39), channel_id=1, source_target_pairs={{0,192},{4,196},{64,0},{68,4},{128,64},{132,68},{192,128},{196,132... | collective-permute-start | bytes 884744 | tf_op jit(solution)/shard_map/ppermute | solution.py:208
  243.5 29.9 %collective-permute-start.15 = (bf16[96,1536]{1,0:T(8,128)(2,1)S(1)}, bf16[96,1536]{1,0:T(8,128)(2,1)S(1)}, u32[]{:S(2)}, u32[]{:S(2)}) collective-permute-start(bf16[96,1536]{1,0:T(8,128)(2,1)S(1)} %get-tuple-element.38), channel_id=1, source_target_pairs={{0,196},{4,0},{64,4},{68,64},{128,68},{132,128},{192,132},{196,192... | collective-permute-start | bytes 884744 | tf_op jit(solution)/shard_map/ppermute | solution.py:208
  288.2 43.6 %copy-start.1 = (bf16[2,4096,16]{1,2,0:T(8,128)(2,1)S(1)}, bf16[2,4096,16]{1,2,0:T(8,128)(2,1)}, u32[]{:S(2)}) copy-start(bf16[2,4096,16]{1,2,0:T(8,128)(2,1)} %param.10) | copy-start | bytes 786436
  (2 other events, 5.0 us)
Sparse Core Ops, SparseCore 0:
  10.3 84.9 all-gather.2
  97.2 54.9 all-gather.4
